TPU v7x, 32 devices: a whole 2x2x4 slice. The times are simulated.
32 devices in a mesh: grp: 2 (over x), spec: 16 (over z, y, core).
Axes of the slice: x: 2, y: 2, z: 4, core: 2. Of those that a mesh axis runs over, the one named last changes fastest.
Arguments:
- spectrum: float32 [3072, 1536], P(('grp', 'spec')), parts along dimension 0, may hold values from 0.05 to 5
- sea_mask: int32 [1536], replicated, may hold values from 0 to 1, as said below
- wind_speed: float32 [3072], P('grp'), parts along dimension 0, may hold values from 0.3 to 3
- wind_angle: float32 [3072], P('grp'), parts along dimension 0, may hold values from -3.140625 to 3.140625
Outputs:
- new_spectrum: float32 [3072, 1536], P(('grp', 'spec')), parts along dimension 0
- wave_height: float32 [3072], P(('grp', 'spec')), parts along dimension 0
- mean_height: float32 [2], P('grp'), parts along dimension 0
There are 2 independent parts, one for each index of `grp`. A program takes and returns all parts, laid end to end along the dimension named above; an argument that names none is the same for every part. Nothing has to cross between parts.
Inputs may be any that keep to these rules, and one draw needn't show every extreme that they name: `sea_mask`: exactly 1024 cells are sea.
All inputs are finite; a program needn't handle non-finite values.
Results may differ from a plain program's by a relative error of at most 0.00002.
Values sent between devices are 32-bit elements; how exact they have to be, the bound alone decides.
A program may use at most 64 MiB of HBM per device.

v0:
```python
import functools
import math

import jax
import jax.numpy as jnp
from jax import lax
from jax.experimental import pallas as pl
from jax.experimental.pallas import tpu as pltpu
from jax.sharding import PartitionSpec as P

NF = 48
ND = 32
NLON = 384
ADV_STEPS = 2
SEA_DEV = 64


def upwind_step(energy, courant_x, courant_y, sea_grid):
    west_cell = jnp.roll(energy, 1, axis=2)
    east_cell = jnp.roll(energy, -1, axis=2)
    edge_row = jnp.zeros_like(energy[:, :1])
    south_cell = jnp.concatenate([edge_row, energy[:, :-1]], axis=1)
    north_cell = jnp.concatenate([energy[:, 1:], edge_row], axis=1)
    updated = (
        energy
        - jnp.maximum(courant_x, 0.0) * (energy - west_cell)
        - jnp.minimum(courant_x, 0.0) * (east_cell - energy)
        - jnp.maximum(courant_y, 0.0) * (energy - south_cell)
        - jnp.minimum(courant_y, 0.0) * (north_cell - energy)
    )
    return updated * sea_grid


def courant_numbers(freq_index, dir_index, lat_count, dir_count):
    speed = 0.2 * jnp.exp(-math.log(1.1) * freq_index)
    heading = 2.0 * math.pi * (dir_index + 0.5) / dir_count
    rows = jnp.arange(lat_count, dtype=jnp.float32)
    latitude = (-75.0 + 150.0 * (rows + 0.5) / lat_count) * (math.pi / 180.0)
    courant_x = (speed * jnp.cos(heading))[:, None, None] / jnp.cos(latitude)[None, :, None]
    courant_y = (speed * jnp.sin(heading))[:, None, None]
    return (courant_x, courant_y)


def shift_freq(values, amount):
    if amount > 0:
        filler = jnp.zeros_like(values[:amount])
        return jnp.concatenate([filler, values[:-amount]], axis=0)
    filler = jnp.zeros_like(values[:-amount])
    return jnp.concatenate([values[-amount:], filler], axis=0)


def source_terms(energy, speed, angle):
    freq_count = energy.shape[0]
    dir_count = energy.shape[1]
    freq_ids = jnp.arange(freq_count, dtype=jnp.float32)
    frequency = jnp.exp(math.log(1.1) * (freq_ids - freq_count // 2))[:, None, None]
    heading = (2.0 * math.pi * (jnp.arange(dir_count, dtype=jnp.float32) + 0.5) / dir_count)[
        None, :, None
    ]
    energy_mean = jnp.mean(energy, axis=(0, 1))
    moment_one = jnp.mean(frequency * energy, axis=(0, 1))
    mean_freq = moment_one / (energy_mean + 1e-06)
    steepness = energy_mean * mean_freq * mean_freq
    breaking = steepness * steepness / (1.0 + steepness * steepness)
    wind_gain = (
        0.05
        * frequency
        * jnp.maximum(
            0.0, speed[None, None, :] * frequency * jnp.cos(heading - angle[None, None, :]) - 1.0
        )
    )
    damping = 0.03 * frequency * breaking[None, None, :]
    valid = ((freq_ids >= 3) & (freq_ids <= freq_count - 3)).astype(jnp.float32)[:, None, None]
    interaction = jnp.zeros_like(energy)
    for mirror in (1, -1):
        plus_bins = shift_freq(jnp.roll(energy, -mirror, axis=1), -2)
        minus_bins = shift_freq(jnp.roll(energy, 3 * mirror, axis=1), 3)
        transfer_rate = (
            0.001
            * valid
            * (energy * energy * (plus_bins + minus_bins) - 2.0 * energy * plus_bins * minus_bins)
        )
        interaction = interaction - 2.0 * transfer_rate
        interaction = interaction + jnp.roll(shift_freq(transfer_rate, 2), mirror, axis=1)
        interaction = interaction + jnp.roll(shift_freq(transfer_rate, -3), -3 * mirror, axis=1)
    updated = energy + (wind_gain - damping) * energy + interaction
    raw_height = 4.0 * jnp.sqrt(jnp.mean(updated, axis=(0, 1)) + 1e-06)
    return (updated, raw_height)


def local(spectrum, sea_mask, wind_speed, wind_angle):
    count = lax.axis_size("spec")
    position = lax.axis_index("spec")
    bins_dev = spectrum.shape[0]
    cells = spectrum.shape[1]
    points = cells // count
    lat_count = cells // NLON
    sea_float = sea_mask.astype(jnp.float32)
    bin_ids = position * bins_dev + jnp.arange(bins_dev, dtype=jnp.int32)
    freq_index = (bin_ids // ND).astype(jnp.float32)
    dir_index = (bin_ids % ND).astype(jnp.float32)
    courant_x, courant_y = courant_numbers(freq_index, dir_index, lat_count, ND)
    sea_grid = sea_float.reshape(1, lat_count, NLON)
    energy = (spectrum * sea_float[None, :]).reshape(bins_dev, lat_count, NLON)
    for substep in range(ADV_STEPS):
        energy = upwind_step(energy, courant_x, courant_y, sea_grid)
    advected = energy.reshape(bins_dev, cells)
    outgoing = advected.reshape(bins_dev, count, points)
    arrived = lax.all_to_all(outgoing, "spec", split_axis=1, concat_axis=0, tiled=True)
    start = position * points
    speed_own = lax.dynamic_slice_in_dim(wind_speed, start, points)
    angle_own = lax.dynamic_slice_in_dim(wind_angle, start, points)
    sea_own = lax.dynamic_slice_in_dim(sea_float, start, points)
    updated, raw_height = source_terms(arrived.reshape(NF, ND, points), speed_own, angle_own)
    wave_height = sea_own * raw_height
    own_total = jnp.zeros((count, 1), jnp.float32) + jnp.sum(wave_height)
    returned, totals = (
        lax.all_to_all(
            updated.reshape(NF * ND, 1, points), "spec", split_axis=0, concat_axis=1, tiled=True
        ),
        lax.all_to_all(own_total, "spec", split_axis=0, concat_axis=1, tiled=True),
    )
    new_spectrum = returned.reshape(bins_dev, cells)
    height_sum = jnp.sum(totals)
    mean_height = (height_sum / (SEA_DEV * count)).reshape(1)
    return (new_spectrum, wave_height, mean_height)


HALO = 5
LANES = 128
WIDE = 256
LAND = 4096.0


def group_size(count, bins_dev, cells):
    size = 4
    if count % size or bins_dev % ND or cells % (size * LANES) or cells % NLON:
        return 0
    if NLON % LANES or bins_dev // ND * size < 2 * HALO or cells % count:
        return 0
    sea = SEA_DEV * count
    if sea > min(cells, LAND) or sea % (size * LANES) or sea % WIDE or cells % WIDE:
        return 0
    if (cells - sea) % WIDE:
        return 0
    return size


def split_bf16(values):
    high = values.astype(jnp.bfloat16)
    left = values - high.astype(jnp.float32)
    mid = left.astype(jnp.bfloat16)
    low = (left - mid.astype(jnp.float32)).astype(jnp.bfloat16)
    return high, mid, low


def rows_of(parts, height, width):
    ids = lax.broadcasted_iota(jnp.int32, (height, width), 0)
    out = jnp.zeros((height, width), jnp.float32)
    for i, part in enumerate(parts):
        out = jnp.where(ids == i, jnp.broadcast_to(part.astype(jnp.float32), (height, width)), out)
    return out.astype(jnp.bfloat16)


def fused_kernel(
    count, group, sea_in, wind_in, angle_in, spec_ref, out_ref, height_ref, spread_ref,
    sea_raw, wind_raw, angle_raw, aux_ref, aux_sem,
    raw, moved, split, pick, wsplit, adv, held, done, mom_out, mom_in, wind, acc, sum_out, sum_in,
    load_sem, held_sem, y_sem, up_sem, down_sem, mom_send, mom_recv,
    ret_send, ret_recv, sum_send, sum_recv,
):
    f32, bf16 = jnp.float32, jnp.bfloat16
    freq_dev, _, sea_cells = adv.shape
    cells = moved.shape[1]
    freq_group = freq_dev * group
    width = sea_cells // group
    zones = count // group
    lat_count = cells // NLON
    sides = group // 2
    parts = width // LANES
    blocks = sea_cells // LANES
    cell_tiles = cells // LANES
    reach = cells - sea_cells + LANES
    me = lax.axis_index("spec")
    zone, rank = me // group, me % group
    side, core = rank // 2, rank % 2

    def remote(src, dst, send, recv, target):
        return pltpu.make_async_remote_copy(
            src_ref=src, dst_ref=dst, send_sem=send, recv_sem=recv,
            device_id={"spec": target}, device_id_type=pl.DeviceIdType.MESH,
        )

    barrier = pltpu.get_barrier_semaphore()
    for step in range(1, count):
        pl.semaphore_signal(
            barrier, inc=1, device_id={"spec": (me + step) % count},
            device_id_type=pl.DeviceIdType.MESH,
        )
    loads = [
        pltpu.make_async_copy(
            spec_ref.at[pl.ds(f * ND, ND)], raw.at[pl.ds(f * ND, ND)], load_sem.at[f]
        )
        for f in range(freq_dev)
    ]
    small = [
        pltpu.make_async_copy(sea_in, sea_raw, aux_sem.at[0]),
        pltpu.make_async_copy(wind_in, wind_raw, aux_sem.at[1]),
        pltpu.make_async_copy(angle_in, angle_raw, aux_sem.at[2]),
    ]
    for load in small[:1] + loads + small[1:]:
        load.start()

    @pl.when(zone == 0)
    def _():
        held[0:HALO] = jnp.zeros((HALO, ND, width), f32)

    @pl.when(zone == zones - 1)
    def _():
        held[HALO + freq_group :] = jnp.zeros((HALO, ND, width), f32)

    def block_of(index, t):
        return t * group + index

    def tile_of(index, t):
        return pl.ds(pl.multiple_of(block_of(index, t) * LANES, LANES), LANES)

    def lanes_of(t):
        return pl.ds(t * LANES, LANES)

    offsets = [(dy, dc) for dy in range(sides) for dc in range(2)]

    def rank_of(offset):
        return (side + offset[0]) % sides * 2 + (core + offset[1]) % 2

    def y_copy(f, i, t):
        peer = rank_of(offsets[i])
        slot = HALO + rank * freq_dev + f
        return remote(
            adv.at[f, :, tile_of(peer, t)], held.at[slot, :, lanes_of(t)],
            y_sem.at[i - 1, f, t], held_sem.at[slot, t], zone * group + peer,
        )

    order = list(range(2, group)) + [1]

    dirs = lax.broadcasted_iota(jnp.int32, (ND, LANES), 0).astype(f32)
    heading = 2.0 * math.pi * (dirs + 0.5) / ND
    cos_h, sin_h = jnp.cos(heading), jnp.sin(heading)
    log_step = math.log(1.1)
    lats = [math.radians(-75.0 + 150.0 * (r + 0.5) / lat_count) for r in range(lat_count)]

    square_rows = lax.broadcasted_iota(jnp.int32, (LANES, LANES), 0)
    square_cols = lax.broadcasted_iota(jnp.int32, (LANES, LANES), 1)
    lane_ids = square_cols.astype(f32)
    ones = jnp.ones((LANES, LANES), bf16)

    small[0].wait()
    aux_ref[...] = sea_raw[...].astype(f32).reshape(1, cells)
    sea = [aux_ref[0:1, r * NLON : (r + 1) * NLON] for r in range(lat_count)]
    mask = [aux_ref[0:1, i * LANES : (i + 1) * LANES] for i in range(cell_tiles)]
    before = [jnp.zeros((1, 1), f32)]
    for i in range(cell_tiles):
        before.append(before[i] + jnp.sum(mask[i], axis=1, keepdims=True))
    for i in range(cell_tiles):
        tri = jnp.where(
            square_cols < square_rows,
            mask[i],
            jnp.where(square_cols == square_rows, LAND * (1.0 - mask[i]), 0.0),
        )
        within = jnp.dot(tri.astype(bf16), ones, preferred_element_type=f32)
        place = within + before[i]
        for b in range(blocks):
            if b <= i and (i - b) * LANES < reach:
                hit = jnp.where(place == lane_ids + float(b * LANES), 1.0, 0.0)
                pick[b, (i - b) * LANES : (i - b + 1) * LANES, :] = hit.astype(bf16)

    quarter = ND // 4
    tiles = NLON // LANES
    mom_out[...] = jnp.zeros_like(mom_out)

    def picked(values, b):
        cols = pl.ds(pl.multiple_of(b * LANES, LANES), reach)
        return jnp.dot(values[:, cols], pick[b], preferred_element_type=f32)

    for f in range(freq_dev):
        loads[f].wait()
        freq = (me * freq_dev + f).astype(f32)
        speed = 0.2 * jnp.exp(jnp.full((quarter, LANES), -log_step, f32) * freq)
        omega = jnp.exp(jnp.full((1, LANES), log_step, f32) * (freq - NF // 2))
        for q in range(4):
            east, north = q in (0, 3), q in (0, 1)
            rows = slice(f * ND + q * quarter, f * ND + (q + 1) * quarter)
            part = slice(q * quarter, (q + 1) * quarter)
            cx0 = speed * jnp.abs(cos_h[part])
            cy = jnp.concatenate([speed * jnp.abs(sin_h[part])] * tiles, axis=1)
            cx = [jnp.concatenate([cx0 * (1.0 / math.cos(a))] * tiles, axis=1) for a in lats]
            energy = [raw[rows, r * NLON : (r + 1) * NLON] * sea[r] for r in range(lat_count)]
            for _ in range(ADV_STEPS):
                fresh = []
                for r in range(lat_count):
                    e = energy[r]
                    side_x = pltpu.roll(e, 1 if east else NLON - 1, 1)
                    other = r - 1 if north else r + 1
                    side_y = energy[other] if 0 <= other < lat_count else 0.0
                    fresh.append((e - cx[r] * (e - side_x) - cy * (e - side_y)) * sea[r])
                energy = fresh
            for r in range(lat_count):
                moved[rows, r * NLON : (r + 1) * NLON] = energy[r]
        for i, piece in enumerate(split_bf16(moved[f * ND : (f + 1) * ND])):
            split[f, i * ND : (i + 1) * ND, :] = piece
        if f == 0:
            pl.semaphore_wait(barrier, count - 1)
        for t in range(parts):
            for i in order + [0]:
                peer = rank_of(offsets[i])
                got = picked(split.at[f], block_of(peer, t))
                got = got[:ND] + got[ND : 2 * ND] + got[2 * ND :]
                if i:
                    adv[f, :, tile_of(peer, t)] = got
                    if t == 0:
                        y_copy(f, i, t).start()
                else:
                    held[HALO + rank * freq_dev + f, :, lanes_of(t)] = got
                total = jnp.sum(got, axis=0, keepdims=True)
                mom_out[0:1, tile_of(peer, t)] += total
                mom_out[1:2, tile_of(peer, t)] += omega * total

    for step in range(1, count):
        target = (me + step) % count
        for t in range(parts):
            remote(
                mom_out.at[:, tile_of(target % group, t)], mom_in.at[me, :, lanes_of(t)],
                mom_send.at[step - 1, t], mom_recv.at[me, t], target,
            ).start()
    for t in range(parts):
        mom_in[me, :, lanes_of(t)] = mom_out[:, tile_of(rank, t)]
    for t in range(1, parts):
        for f in range(freq_dev):
            for i in order:
                y_copy(f, i, t).start()

    small[1].wait()
    small[2].wait()
    speed_all = wind_raw[...].reshape(1, cells)
    angle_all = angle_raw[...].reshape(1, cells)
    wsplit[...] = rows_of(
        split_bf16(speed_all * jnp.cos(angle_all)) + split_bf16(speed_all * jnp.sin(angle_all)),
        2 * quarter, cells,
    )
    for t in range(parts):
        own = picked(wsplit, block_of(rank, t))
        along = own[0:1] + own[1:2] + own[2:3]
        across = own[3:4] + own[4:5] + own[5:6]
        wind[:, t * LANES : (t + 1) * LANES] = cos_h * along + sin_h * across

    tri_up = jnp.where(square_rows < square_cols, 1.0, 0.0).astype(bf16)
    ranks = jnp.dot(
        rows_of(mask, 2 * quarter, LANES), tri_up, preferred_element_type=f32
    )
    places = [
        jnp.where(mask[i] > 0.0, ranks[i : i + 1] + before[i], LAND) for i in range(cell_tiles)
    ]
    wide_rows = lax.broadcasted_iota(jnp.int32, (WIDE, LANES), 0).astype(f32)
    for j in range(cells // WIDE):
        for u in range(sea_cells // WIDE):
            if u * WIDE < (j + 1) * WIDE and (u + 1) * WIDE > j * WIDE - (cells - sea_cells):
                for h in range(WIDE // LANES):
                    i = j * (WIDE // LANES) + h
                    hit = jnp.where(wide_rows + float(u * WIDE) == places[i], 1.0, 0.0)
                    spread_ref[
                        u * WIDE : (u + 1) * WIDE, i * LANES : (i + 1) * LANES
                    ] = hit.astype(bf16)

    def up_copy(slot, t):
        return remote(
            held.at[HALO + slot, :, lanes_of(t)],
            held.at[HALO + slot - freq_group, :, lanes_of(t)],
            up_sem.at[slot - (freq_group - HALO), t],
            held_sem.at[HALO + slot - freq_group, t],
            (zone + 1) % zones * group + rank,
        )

    def down_copy(slot, t):
        return remote(
            held.at[HALO + slot, :, lanes_of(t)],
            held.at[HALO + slot + freq_group, :, lanes_of(t)],
            down_sem.at[slot, t],
            held_sem.at[HALO + slot + freq_group, t],
            (zone + zones - 1) % zones * group + rank,
        )

    def arrive(index, t):
        block = held.at[index, :, lanes_of(t)]
        remote(
            block, block, up_sem.at[0, t], held_sem.at[index, t], (me + 1) % count
        ).wait_recv()

    def arrive_group(dy, t):
        for f in range(freq_dev):
            for dc in range(2):
                slot = rank_of((dy, dc)) * freq_dev + f
                if (dy, dc) != (0, 0):
                    arrive(HALO + slot, t)

                @pl.when((slot >= freq_group - HALO) & (zone < zones - 1))
                def _():
                    up_copy(slot, t).start()

                @pl.when((slot < HALO) & (zone > 0))
                def _():
                    down_copy(slot, t).start()

    for t in range(parts):
        arrive_group(0, t)
    for dy in range(1, sides):
        arrive_group(dy, 0)

    for step in range(1, count):
        source = (me + step) % count
        for t in range(parts):
            block = mom_in.at[source, :, lanes_of(t)]
            remote(
                block, block, mom_send.at[0, t], mom_recv.at[source, t], source
            ).wait_recv()
    total = jnp.sum(mom_in[...], axis=0) * (1.0 / (NF * ND))
    energy_mean, moment_one = total[0:1], total[1:2]
    mean_freq = moment_one / (energy_mean + 1e-06)
    steepness = energy_mean * mean_freq * mean_freq
    breaking = steepness * steepness / (1.0 + steepness * steepness)

    acc[...] = jnp.zeros_like(acc)
    ascending = side > 0

    def arrive_halo(at_top, t):
        @pl.when(jnp.where(at_top, zone < zones - 1, zone > 0))
        def _():
            for i in range(HALO):
                arrive(jnp.where(at_top, HALO + freq_group + i, i), t)

    def ret_copy(owner, t):
        return remote(
            done.at[pl.ds(owner * freq_dev, freq_dev), :, lanes_of(t)],
            out_ref.at[:, :, tile_of(rank, t)],
            ret_send.at[owner, t], ret_recv.at[rank, t], zone * group + owner,
        )

    def sources(t, begin, end):
        lanes = slice(t * LANES, (t + 1) * LANES)

        def source_step(i, carry):
            k = jnp.where(ascending, i, freq_group - 1 - i)
            freq = zone * freq_group + k

            def scale(index, factor):
                return jnp.where((index >= 3) & (index <= NF - 3), factor, 0.0).astype(f32)

            w_own = scale(freq, -0.002)
            w_low, w_high = scale(freq - 2, 0.001), scale(freq + 3, 0.001)
            omega = jnp.exp(
                jnp.full((1, LANES), log_step, f32) * (freq.astype(f32) - NF // 2)
            )

            def slab(shift):
                return held[HALO + k + shift, :, lanes]

            def turn(values, amount):
                return pltpu.roll(values, amount % ND, 0)

            def rate(a, p, m):
                return a * (a * (p + m) - 2.0 * (p * m))

            own = slab(0)
            p2, m3, m2, m5, p3, p5 = (slab(shift) for shift in (2, -3, -2, -5, 3, 5))
            near = rate(own, turn(p2, -1), turn(m3, 3)) + rate(own, turn(p2, 1), turn(m3, -3))
            low = rate(turn(m2, 1), own, turn(m5, 4)) + rate(turn(m2, -1), own, turn(m5, -4))
            high = rate(turn(p3, -3), turn(p5, -4), own) + rate(turn(p3, 3), turn(p5, 4), own)
            interaction = w_own * near + w_low * low + w_high * high
            gain = (0.05 * omega) * jnp.maximum(0.0, wind[:, lanes] * omega - 1.0)
            damping = (0.03 * omega) * breaking[:, lanes]
            fresh = own + (gain - damping) * own + interaction
            done[k, :, lanes] = fresh
            acc[:, lanes] += fresh
            return carry

        lax.fori_loop(begin, end, source_step, 0)

    half = freq_group // 2
    near_side = rank_of((0, 1))

    def first_half(t):
        arrive_halo(jnp.logical_not(ascending), t)
        sources(t, 0, half)
        for dy in range(1, sides):
            for dc in range(2):
                ret_copy(rank_of((dy, dc)), t).start()

    def second_half(t):
        arrive_halo(ascending, t)
        sources(t, half, freq_group)
        ret_copy(near_side, t).start()
        out_ref[:, :, tile_of(rank, t)] = done[
            pl.ds(rank * freq_dev, freq_dev), :, lanes_of(t)
        ]

    first_half(0)
    for t in range(1, parts):
        for dy in range(1, sides):
            arrive_group(dy, t)
        first_half(t)
        second_half(t - 1)
    second_half(parts - 1)

    sum_out[...] = jnp.sum(acc[...], axis=0, keepdims=True)

    def sum_copy(step):
        return remote(
            sum_out, sum_in.at[me], sum_send.at[step - 1], sum_recv.at[me], (me + step) % count
        )

    for step in range(1, count):
        sum_copy(step).start()
    sum_in[me] = sum_out[...]
    for step in range(1, count):
        source = (me + step) % count
        remote(
            sum_out, sum_in.at[source], sum_send.at[0], sum_recv.at[source], source
        ).wait_recv()

    for g in range(group):
        mass = sum_in[g]
        for other in range(1, zones):
            mass = mass + sum_in[other * group + g]
        height = 4.0 * jnp.sqrt(mass * (1.0 / (NF * ND)) + 1e-06)
        for t in range(parts):
            height_ref[0:1, block_of(g, t) * LANES : (block_of(g, t) + 1) * LANES] = height[
                :, t * LANES : (t + 1) * LANES
            ]

    for t in range(parts):
        for i in range(1, group):
            peer = rank_of(offsets[i])
            remote(
                done.at[pl.ds(0, freq_dev), :, lanes_of(t)], out_ref.at[:, :, tile_of(peer, t)],
                ret_send.at[peer, t], ret_recv.at[peer, t], zone * group + peer,
            ).wait_recv()
            for f in range(freq_dev):
                y_copy(f, i, t).wait_send()
            ret_copy(peer, t).wait_send()
    for step in range(1, count):
        for t in range(parts):
            remote(
                mom_out.at[:, tile_of(0, t)], mom_in.at[me, :, lanes_of(t)],
                mom_send.at[step - 1, t], mom_recv.at[me, t], (me + step) % count,
            ).wait_send()
        sum_copy(step).wait_send()

    @pl.when(zone < zones - 1)
    def _():
        for t in range(parts):
            for slot in range(freq_group - HALO, freq_group):
                up_copy(slot, t).wait_send()

    @pl.when(zone > 0)
    def _():
        for t in range(parts):
            for slot in range(HALO):
                down_copy(slot, t).wait_send()


def store_kernel(
    count, new_in, height_in, spread_in, new_out, wave_ref, mean_ref, split, full, tall, sem
):
    rows, cells = full.shape
    sea_cells = height_in.shape[1]
    land = cells - sea_cells
    f32 = jnp.float32
    me = lax.axis_index("spec")
    height = height_in[...]
    mean_ref[...] = jnp.sum(height, axis=1, keepdims=True) * (1.0 / sea_cells)
    for i, piece in enumerate(split_bf16(new_in[...].reshape(rows, sea_cells))):
        split[i * rows : (i + 1) * rows, :] = piece
    split[3 * rows :, :] = rows_of(split_bf16(height), split.shape[0] - 3 * rows, sea_cells)
    copies = []
    for j in range(cells // WIDE):
        low, high = max(0, j * WIDE - land), min(sea_cells, (j + 1) * WIDE)
        cols = slice(j * WIDE, (j + 1) * WIDE)
        got = jnp.dot(
            split[:, low:high], spread_in[low:high, cols], preferred_element_type=f32
        )
        full[:, cols] = got[:rows] + got[rows : 2 * rows] + got[2 * rows : 3 * rows]
        tall[:, cols] = got[3 * rows : 3 * rows + 1] + got[3 * rows + 1 : 3 * rows + 2] + (
            got[3 * rows + 2 : 3 * rows + 3]
        )
        copy = pltpu.make_async_copy(full.at[:, cols], new_out.at[:, cols], sem.at[j])
        copy.start()
        copies.append(copy)
    points = cells // count
    row = LANES * points // math.gcd(LANES, points)
    per_row = row // points
    mine = tall[:, pl.ds(pl.multiple_of(me // per_row * row, LANES), row)]
    shift = (me % per_row) * points
    turned = pltpu.roll(jnp.broadcast_to(mine, (8, row)), (row - shift) % row, 1)
    wave_ref[...] = turned[0, :points]
    for copy in copies:
        copy.wait()


def fused_local(spectrum, sea_mask, wind_speed, wind_angle):
    count = lax.axis_size("spec")
    bins_dev, cells = spectrum.shape
    group = group_size(count, bins_dev, cells)
    freq_dev = bins_dev // ND
    freq_group = freq_dev * group
    sea_cells = SEA_DEV * count
    width = sea_cells // group
    points = cells // count
    parts = width // LANES
    blocks = sea_cells // LANES
    reach = cells - sea_cells + LANES
    tail = 16
    f32, bf16 = jnp.float32, jnp.bfloat16
    dma = pltpu.SemaphoreType.DMA
    vmem = pl.BlockSpec(memory_space=pltpu.VMEM)
    handed = pl.pallas_call(
        functools.partial(fused_kernel, count, group),
        out_shape=(
            pltpu.VMEM((freq_dev, ND, sea_cells), f32),
            pltpu.VMEM((1, sea_cells), f32),
            pltpu.VMEM((sea_cells, cells), bf16),
        ),
        in_specs=[pl.BlockSpec(memory_space=pl.ANY)] * 4,
        out_specs=(vmem,) * 3,
        scratch_shapes=[
            pltpu.VMEM((cells,), jnp.int32),
            pltpu.VMEM((cells,), f32),
            pltpu.VMEM((cells,), f32),
            pltpu.VMEM((1, cells), f32),
            dma((3,)),
            pltpu.VMEM((bins_dev, cells), f32),
            pltpu.VMEM((bins_dev, cells), f32),
            pltpu.VMEM((freq_dev, 3 * ND, cells), bf16),
            pltpu.VMEM((blocks, reach, LANES), bf16),
            pltpu.VMEM((ND // 2, cells), bf16),
            pltpu.VMEM((freq_dev, ND, sea_cells), f32),
            pltpu.VMEM((freq_group + 2 * HALO, ND, width), f32),
            pltpu.VMEM((freq_group, ND, width), f32),
            pltpu.VMEM((2, sea_cells), f32),
            pltpu.VMEM((count, 2, width), f32),
            pltpu.VMEM((ND, width), f32),
            pltpu.VMEM((ND, width), f32),
            pltpu.VMEM((1, width), f32),
            pltpu.VMEM((count, 1, width), f32),
            dma((freq_dev,)),
            dma((freq_group + 2 * HALO, parts)),
            dma((group - 1, freq_dev, parts)),
            dma((HALO, parts)),
            dma((HALO, parts)),
            dma((count - 1, parts)),
            dma((count, parts)),
            dma((group, parts)),
            dma((group, parts)),
            dma((count - 1,)),
            dma((count,)),
        ],
        compiler_params=pltpu.CompilerParams(collective_id=0, has_side_effects=True),
    )(sea_mask, wind_speed, wind_angle, spectrum)
    out, wave, mean = pl.pallas_call(
        functools.partial(store_kernel, count),
        out_shape=(
            pltpu.HBM((bins_dev, cells), f32),
            jax.ShapeDtypeStruct((points,), f32),
            jax.ShapeDtypeStruct((1, 1), f32),
        ),
        in_specs=[vmem] * 3,
        out_specs=(pl.BlockSpec(memory_space=pltpu.HBM), vmem, vmem),
        scratch_shapes=[
            pltpu.VMEM((3 * bins_dev + tail, sea_cells), bf16),
            pltpu.VMEM((bins_dev, cells), f32),
            pltpu.VMEM((1, cells), f32),
            dma((cells // WIDE,)),
        ],
    )(*[pltpu.with_memory_space_constraint(piece, pltpu.VMEM) for piece in handed])
    return (out, wave, mean.reshape(1))


def solution(mesh):
    in_specs = (P(("grp", "spec"), None), P(), P("grp"), P("grp"))
    out_specs = (P(("grp", "spec"), None), P(("grp", "spec")), P("grp"))

    def body(spectrum, sea_mask, wind_speed, wind_angle):
        fits = group_size(mesh.shape["spec"], *spectrum.shape)
        plan = fused_local if fits else local
        return plan(spectrum, sea_mask, wind_speed, wind_angle)

    return jax.shard_map(body, mesh=mesh, in_specs=in_specs, out_specs=out_specs, check_vma=False)
```

profile of v0, /device:TPU:0, one launch (start us, length us, event | category | flops | bytes accessed | tf_op | source)
XLA Modules:
  0.0 26.1 jit_solution(12568782361841399218)
XLA Ops:
  0.6 23.6 %shard_map.67 = (f32[3,32,1024]{2,1,0:T(8,128)S(1)}, f32[1,1024]{1,0:T(1,128)S(1)}, bf16[1024,1536]{1,0:T(8,128)(2,1)S(1)}) custom-call(s32[1536]{0:T(1024)} %sea_in.1, f32[1536]{0:T(1024)} %wind_in.1, f32[1536]{0:T(1024)} %angle_in.1, f32[96,1536]{1,0:T(8,128)} %spec_ref.1), custom_call_target="tpu_custom_call" | custom-call | tf_op jit(solution)/shard_map/pallas_call | solution.py:624
  24.2 1.9 %shard_map.68 = (f32[96,1536]{1,0:T(8,128)}, f32[96]{0:T(128)}, f32[1,1]{1,0:T(1,128)}) custom-call(f32[3,32,1024]{2,1,0:T(8,128)S(1)} %get-tuple-element.9.new_in, f32[1,1024]{1,0:T(1,128)S(1)} %get-tuple-element.10.height_in, bf16[1024,1536]{1,0:T(8,128)(2,1)S(1)} %get-tuple-element.11.spread_in), custom_call_target="tpu_custom_call" | custom-call | tf_op jit(solution)/shard_map/pallas_call | solution.py:667
where the time goes:
time: 26.3 us; the launch traced here: 26.1 us
  Pallas kernels  25.5 us (97%)
  between operations  0.64 us (2%)
    pallas_call x1, Pallas kernels, fused_local(): pl.pallas_call(functools.partial(fused_kernel, count, group), out_shape=(...  23.6 us
    pallas_call x1, Pallas kernels, fused_local(): pl.pallas_call(functools.partial(store_kernel, count), out_shape=(pltpu.H...  1.9 us

commit v1 on v0

--- a/solution.py
+++ b/solution.py
@@ -163,24 +163,25 @@
 
 
 def fused_kernel(
-    count, group, sea_in, wind_in, angle_in, spec_ref, out_ref, height_ref, spread_ref,
+    count, group, sea_in, wind_in, angle_in, spec_ref, full_ref, height_ref, spread_ref,
     sea_raw, wind_raw, angle_raw, aux_ref, aux_sem,
-    raw, moved, split, pick, wsplit, adv, held, done, mom_out, mom_in, wind, acc, sum_out, sum_in,
-    load_sem, held_sem, y_sem, up_sem, down_sem, mom_send, mom_recv,
-    ret_send, ret_recv, sum_send, sum_recv,
+    raw, moved, split, pick, wsplit, adv, held, done, back, mom_out, mom_in, wind, acc,
+    sum_out, sum_in, damp_out, damp_in,
+    load_sem, held_sem, halo_sem, y_sem, z_sem, mom_send, mom_recv,
+    ret_send, ret_recv, sum_send, sum_recv, damp_send, damp_recv,
 ):
     f32, bf16 = jnp.float32, jnp.bfloat16
     freq_dev, _, sea_cells = adv.shape
-    cells = moved.shape[1]
+    bins_dev, cells = moved.shape
     freq_group = freq_dev * group
     width = sea_cells // group
     zones = count // group
     lat_count = cells // NLON
     sides = group // 2
     parts = width // LANES
-    blocks = sea_cells // LANES
     cell_tiles = cells // LANES
-    reach = cells - sea_cells + LANES
+    land = cells - sea_cells
+    reach = land + WIDE
     me = lax.axis_index("spec")
     zone, rank = me // group, me % group
     side, core = rank // 2, rank % 2
@@ -191,12 +192,6 @@
             device_id={"spec": target}, device_id_type=pl.DeviceIdType.MESH,
         )
 
-    barrier = pltpu.get_barrier_semaphore()
-    for step in range(1, count):
-        pl.semaphore_signal(
-            barrier, inc=1, device_id={"spec": (me + step) % count},
-            device_id_type=pl.DeviceIdType.MESH,
-        )
     loads = [
         pltpu.make_async_copy(
             spec_ref.at[pl.ds(f * ND, ND)], raw.at[pl.ds(f * ND, ND)], load_sem.at[f]
@@ -210,6 +205,12 @@
     ]
     for load in small[:1] + loads + small[1:]:
         load.start()
+    barrier = pltpu.get_barrier_semaphore()
+    for step in range(1, count):
+        pl.semaphore_signal(
+            barrier, inc=1, device_id={"spec": (me + step) % count},
+            device_id_type=pl.DeviceIdType.MESH,
+        )
 
     @pl.when(zone == 0)
     def _():
@@ -238,16 +239,17 @@
         slot = HALO + rank * freq_dev + f
         return remote(
             adv.at[f, :, tile_of(peer, t)], held.at[slot, :, lanes_of(t)],
-            y_sem.at[i - 1, f, t], held_sem.at[slot, t], zone * group + peer,
-        )
-
-    order = list(range(2, group)) + [1]
+            y_sem, held_sem.at[slot, t], zone * group + peer,
+        )
 
     dirs = lax.broadcasted_iota(jnp.int32, (ND, LANES), 0).astype(f32)
     heading = 2.0 * math.pi * (dirs + 0.5) / ND
     cos_h, sin_h = jnp.cos(heading), jnp.sin(heading)
     log_step = math.log(1.1)
     lats = [math.radians(-75.0 + 150.0 * (r + 0.5) / lat_count) for r in range(lat_count)]
+
+    def omega_of(freq, shape):
+        return jnp.exp(jnp.full(shape, log_step, f32) * (freq.astype(f32) - NF // 2))
 
     square_rows = lax.broadcasted_iota(jnp.int32, (LANES, LANES), 0)
     square_cols = lax.broadcasted_iota(jnp.int32, (LANES, LANES), 1)
@@ -269,24 +271,20 @@
         )
         within = jnp.dot(tri.astype(bf16), ones, preferred_element_type=f32)
         place = within + before[i]
-        for b in range(blocks):
-            if b <= i and (i - b) * LANES < reach:
-                hit = jnp.where(place == lane_ids + float(b * LANES), 1.0, 0.0)
-                pick[b, (i - b) * LANES : (i - b + 1) * LANES, :] = hit.astype(bf16)
+        for p in range(sea_cells // WIDE):
+            row = i * LANES - p * WIDE
+            if 0 <= row < reach:
+                for h in range(WIDE // LANES):
+                    first = float(p * WIDE + h * LANES)
+                    hit = jnp.where(place == lane_ids + first, 1.0, 0.0)
+                    pick[p, row : row + LANES, h * LANES : (h + 1) * LANES] = hit.astype(bf16)
 
     quarter = ND // 4
     tiles = NLON // LANES
-    mom_out[...] = jnp.zeros_like(mom_out)
-
-    def picked(values, b):
-        cols = pl.ds(pl.multiple_of(b * LANES, LANES), reach)
-        return jnp.dot(values[:, cols], pick[b], preferred_element_type=f32)
-
     for f in range(freq_dev):
         loads[f].wait()
         freq = (me * freq_dev + f).astype(f32)
         speed = 0.2 * jnp.exp(jnp.full((quarter, LANES), -log_step, f32) * freq)
-        omega = jnp.exp(jnp.full((1, LANES), log_step, f32) * (freq - NF // 2))
         for q in range(4):
             east, north = q in (0, 3), q in (0, 1)
             rows = slice(f * ND + q * quarter, f * ND + (q + 1) * quarter)
@@ -306,38 +304,52 @@
                 energy = fresh
             for r in range(lat_count):
                 moved[rows, r * NLON : (r + 1) * NLON] = energy[r]
-        for i, piece in enumerate(split_bf16(moved[f * ND : (f + 1) * ND])):
-            split[f, i * ND : (i + 1) * ND, :] = piece
-        if f == 0:
-            pl.semaphore_wait(barrier, count - 1)
-        for t in range(parts):
-            for i in order + [0]:
-                peer = rank_of(offsets[i])
-                got = picked(split.at[f], block_of(peer, t))
-                got = got[:ND] + got[ND : 2 * ND] + got[2 * ND :]
-                if i:
-                    adv[f, :, tile_of(peer, t)] = got
-                    if t == 0:
-                        y_copy(f, i, t).start()
-                else:
-                    held[HALO + rank * freq_dev + f, :, lanes_of(t)] = got
-                total = jnp.sum(got, axis=0, keepdims=True)
-                mom_out[0:1, tile_of(peer, t)] += total
-                mom_out[1:2, tile_of(peer, t)] += omega * total
+        rows = slice(f * ND, (f + 1) * ND)
+        for i, piece in enumerate(split_bf16(moved[rows])):
+            split[i * bins_dev + f * ND : i * bins_dev + (f + 1) * ND, :] = piece
+
+    pl.semaphore_wait(barrier, count - 1)
+
+    def packed(values, pair):
+        cols = pl.ds(pl.multiple_of(pair * WIDE, LANES), reach)
+        return jnp.dot(values[:, cols], pick[pair], preferred_element_type=f32)
+
+    for t in range(parts):
+        for dy in list(range(1, sides)) + [0]:
+            pair = t * sides + (side + dy) % sides
+            got = packed(split, pair)
+            got = got[:bins_dev] + got[bins_dev : 2 * bins_dev] + got[2 * bins_dev :]
+            cols = pl.ds(pl.multiple_of(pair * WIDE, LANES), WIDE)
+            mass, moment = None, None
+            for f in range(freq_dev):
+                piece = got[f * ND : (f + 1) * ND]
+                adv[f, :, cols] = piece
+                total = jnp.sum(piece, axis=0, keepdims=True)
+                scaled = omega_of(me * freq_dev + f, (1, WIDE)) * total
+                mass = total if f == 0 else mass + total
+                moment = scaled if f == 0 else moment + scaled
+            for f in range(freq_dev):
+                for dc in ((0, 1) if dy else (1,)):
+                    y_copy(f, dy * 2 + dc, t).start()
+            if dy == 0:
+                for f in range(freq_dev):
+                    held[HALO + rank * freq_dev + f, :, lanes_of(t)] = adv[
+                        f, :, tile_of(rank, t)
+                    ]
+            here = pl.ds(pl.multiple_of((side + dy) % sides * WIDE, LANES), WIDE)
+            mom_out[t, 0:1, here] = mass
+            mom_out[t, 1:2, here] = moment
+
+    def cols_of(index):
+        return pl.ds(pl.multiple_of(index * LANES, LANES), LANES)
 
     for step in range(1, count):
         target = (me + step) % count
-        for t in range(parts):
-            remote(
-                mom_out.at[:, tile_of(target % group, t)], mom_in.at[me, :, lanes_of(t)],
-                mom_send.at[step - 1, t], mom_recv.at[me, t], target,
-            ).start()
-    for t in range(parts):
-        mom_in[me, :, lanes_of(t)] = mom_out[:, tile_of(rank, t)]
-    for t in range(1, parts):
-        for f in range(freq_dev):
-            for i in order:
-                y_copy(f, i, t).start()
+        remote(
+            mom_out.at[:, :, cols_of(target % group)], mom_in.at[me],
+            mom_send, mom_recv, target,
+        ).start()
+    mom_in[me] = mom_out[:, :, cols_of(rank)]
 
     small[1].wait()
     small[2].wait()
@@ -348,10 +360,47 @@
         2 * quarter, cells,
     )
     for t in range(parts):
-        own = picked(wsplit, block_of(rank, t))
+        own = packed(wsplit, t * sides + side)
+        own = jnp.where(core == 0, own[:, :LANES], own[:, LANES:])
         along = own[0:1] + own[1:2] + own[2:3]
         across = own[3:4] + own[4:5] + own[5:6]
         wind[:, t * LANES : (t + 1) * LANES] = cos_h * along + sin_h * across
+
+    def up_copy(slot, t):
+        return remote(
+            held.at[HALO + slot, :, lanes_of(t)],
+            held.at[HALO + slot - freq_group, :, lanes_of(t)],
+            z_sem.at[0], halo_sem.at[0, t], (zone + 1) % zones * group + rank,
+        )
+
+    def down_copy(slot, t):
+        return remote(
+            held.at[HALO + slot, :, lanes_of(t)],
+            held.at[HALO + slot + freq_group, :, lanes_of(t)],
+            z_sem.at[1], halo_sem.at[1, t], (zone + zones - 1) % zones * group + rank,
+        )
+
+    def arrive(index, t):
+        block = held.at[index, :, lanes_of(t)]
+        remote(block, block, y_sem, held_sem.at[index, t], (me + 1) % count).wait_recv()
+
+    def arrive_group(dy, t):
+        for f in range(freq_dev):
+            for dc in range(2):
+                slot = rank_of((dy, dc)) * freq_dev + f
+                if (dy, dc) != (0, 0):
+                    arrive(HALO + slot, t)
+
+                @pl.when((slot >= freq_group - HALO) & (zone < zones - 1))
+                def _():
+                    up_copy(slot, t).start()
+
+                @pl.when((slot < HALO) & (zone > 0))
+                def _():
+                    down_copy(slot, t).start()
+
+    for t in range(parts):
+        arrive_group(0, t)
 
     tri_up = jnp.where(square_rows < square_cols, 1.0, 0.0).astype(bf16)
     ranks = jnp.dot(
@@ -361,87 +410,39 @@
         jnp.where(mask[i] > 0.0, ranks[i : i + 1] + before[i], LAND) for i in range(cell_tiles)
     ]
     wide_rows = lax.broadcasted_iota(jnp.int32, (WIDE, LANES), 0).astype(f32)
-    for j in range(cells // WIDE):
-        for u in range(sea_cells // WIDE):
-            if u * WIDE < (j + 1) * WIDE and (u + 1) * WIDE > j * WIDE - (cells - sea_cells):
-                for h in range(WIDE // LANES):
-                    i = j * (WIDE // LANES) + h
-                    hit = jnp.where(wide_rows + float(u * WIDE) == places[i], 1.0, 0.0)
-                    spread_ref[
-                        u * WIDE : (u + 1) * WIDE, i * LANES : (i + 1) * LANES
-                    ] = hit.astype(bf16)
-
-    def up_copy(slot, t):
-        return remote(
-            held.at[HALO + slot, :, lanes_of(t)],
-            held.at[HALO + slot - freq_group, :, lanes_of(t)],
-            up_sem.at[slot - (freq_group - HALO), t],
-            held_sem.at[HALO + slot - freq_group, t],
-            (zone + 1) % zones * group + rank,
-        )
-
-    def down_copy(slot, t):
-        return remote(
-            held.at[HALO + slot, :, lanes_of(t)],
-            held.at[HALO + slot + freq_group, :, lanes_of(t)],
-            down_sem.at[slot, t],
-            held_sem.at[HALO + slot + freq_group, t],
-            (zone + zones - 1) % zones * group + rank,
-        )
-
-    def arrive(index, t):
-        block = held.at[index, :, lanes_of(t)]
-        remote(
-            block, block, up_sem.at[0, t], held_sem.at[index, t], (me + 1) % count
-        ).wait_recv()
-
-    def arrive_group(dy, t):
-        for f in range(freq_dev):
-            for dc in range(2):
-                slot = rank_of((dy, dc)) * freq_dev + f
-                if (dy, dc) != (0, 0):
-                    arrive(HALO + slot, t)
-
-                @pl.when((slot >= freq_group - HALO) & (zone < zones - 1))
-                def _():
-                    up_copy(slot, t).start()
-
-                @pl.when((slot < HALO) & (zone > 0))
-                def _():
-                    down_copy(slot, t).start()
-
-    for t in range(parts):
-        arrive_group(0, t)
+    for u in range(sea_cells // WIDE):
+        for i in range(cell_tiles):
+            if u * WIDE < (i + 1) * LANES + LANES and (u + 1) * WIDE + LANES > i * LANES - land:
+                hit = jnp.where(wide_rows + float(u * WIDE) == places[i], 1.0, 0.0)
+                spread_ref[u * WIDE : (u + 1) * WIDE, i * LANES : (i + 1) * LANES] = hit.astype(
+                    bf16
+                )
+            else:
+                spread_ref[u * WIDE : (u + 1) * WIDE, i * LANES : (i + 1) * LANES] = jnp.zeros(
+                    (WIDE, LANES), bf16
+                )
+
     for dy in range(1, sides):
         arrive_group(dy, 0)
 
-    for step in range(1, count):
-        source = (me + step) % count
-        for t in range(parts):
-            block = mom_in.at[source, :, lanes_of(t)]
-            remote(
-                block, block, mom_send.at[0, t], mom_recv.at[source, t], source
-            ).wait_recv()
-    total = jnp.sum(mom_in[...], axis=0) * (1.0 / (NF * ND))
-    energy_mean, moment_one = total[0:1], total[1:2]
-    mean_freq = moment_one / (energy_mean + 1e-06)
-    steepness = energy_mean * mean_freq * mean_freq
-    breaking = steepness * steepness / (1.0 + steepness * steepness)
-
     acc[...] = jnp.zeros_like(acc)
     ascending = side > 0
 
     def arrive_halo(at_top, t):
+        block = held.at[0:HALO, :, lanes_of(t)]
+
         @pl.when(jnp.where(at_top, zone < zones - 1, zone > 0))
         def _():
-            for i in range(HALO):
-                arrive(jnp.where(at_top, HALO + freq_group + i, i), t)
+            way = jnp.where(at_top, 1, 0)
+            remote(
+                block, block, z_sem.at[0], halo_sem.at[way, t], (me + 1) % count
+            ).wait_recv()
 
     def ret_copy(owner, t):
         return remote(
             done.at[pl.ds(owner * freq_dev, freq_dev), :, lanes_of(t)],
-            out_ref.at[:, :, tile_of(rank, t)],
-            ret_send.at[owner, t], ret_recv.at[rank, t], zone * group + owner,
+            back.at[:, :, tile_of(rank, t)],
+            ret_send, ret_recv.at[t], zone * group + owner,
         )
 
     def sources(t, begin, end):
@@ -456,9 +457,7 @@
 
             w_own = scale(freq, -0.002)
             w_low, w_high = scale(freq - 2, 0.001), scale(freq + 3, 0.001)
-            omega = jnp.exp(
-                jnp.full((1, LANES), log_step, f32) * (freq.astype(f32) - NF // 2)
-            )
+            omega = omega_of(freq, (1, LANES))
 
             def slab(shift):
                 return held[HALO + k + shift, :, lanes]
@@ -476,8 +475,7 @@
             high = rate(turn(p3, -3), turn(p5, -4), own) + rate(turn(p3, 3), turn(p5, 4), own)
             interaction = w_own * near + w_low * low + w_high * high
             gain = (0.05 * omega) * jnp.maximum(0.0, wind[:, lanes] * omega - 1.0)
-            damping = (0.03 * omega) * breaking[:, lanes]
-            fresh = own + (gain - damping) * own + interaction
+            fresh = own + gain * own + interaction
             done[k, :, lanes] = fresh
             acc[:, lanes] += fresh
             return carry
@@ -498,111 +496,119 @@
         arrive_halo(ascending, t)
         sources(t, half, freq_group)
         ret_copy(near_side, t).start()
-        out_ref[:, :, tile_of(rank, t)] = done[
+        back[:, :, tile_of(rank, t)] = done[
             pl.ds(rank * freq_dev, freq_dev), :, lanes_of(t)
         ]
+
+    def zone_copy(dst_rank, src, dst, send, recv):
+        return remote(src, dst, send, recv, zone * group + dst_rank)
+
+    def damping_terms():
+        others = mom_in.at[0 : count - 1]
+        remote(others, others, mom_send, mom_recv, (me + 1) % count).wait_recv()
+        total = jnp.sum(mom_in[...], axis=0) * (1.0 / (NF * ND))
+        for t in range(parts):
+            energy_mean, moment_one = total[t, 0:1], total[t, 1:2]
+            mean_freq = moment_one / (energy_mean + 1e-06)
+            steepness = energy_mean * mean_freq * mean_freq
+            breaking = steepness * steepness / (1.0 + steepness * steepness)
+            damp_out[t, 0:1] = 0.03 * breaking
+            damp_out[t, 1:2] = 0.03 * breaking * moment_one
+        for i in range(1, group):
+            zone_copy(
+                rank_of(offsets[i]), damp_out, damp_in.at[rank], damp_send, damp_recv
+            ).start()
+        damp_in[rank] = damp_out[...]
 
     first_half(0)
     for t in range(1, parts):
         for dy in range(1, sides):
             arrive_group(dy, t)
         first_half(t)
+        if t == parts - 1:
+            damping_terms()
         second_half(t - 1)
     second_half(parts - 1)
 
     sum_out[...] = jnp.sum(acc[...], axis=0, keepdims=True)
-
-    def sum_copy(step):
-        return remote(
-            sum_out, sum_in.at[me], sum_send.at[step - 1], sum_recv.at[me], (me + step) % count
-        )
-
     for step in range(1, count):
-        sum_copy(step).start()
+        remote(sum_out, sum_in.at[me], sum_send, sum_recv, (me + step) % count).start()
     sum_in[me] = sum_out[...]
-    for step in range(1, count):
-        source = (me + step) % count
-        remote(
-            sum_out, sum_in.at[source], sum_send.at[0], sum_recv.at[source], source
-        ).wait_recv()
-
+
+    others = damp_in.at[0 : group - 1]
+    remote(others, others, damp_send, damp_recv, (me + 1) % count).wait_recv()
+    for t in range(parts):
+        block = done.at[0 : (group - 1) * freq_dev, :, lanes_of(t)]
+        remote(block, block, ret_send, ret_recv.at[t], (me + 1) % count).wait_recv()
+    for f in range(freq_dev):
+        omega = omega_of(me * freq_dev + f, (1, LANES))
+        for t in range(parts):
+            for g in range(group):
+                cols = slice(block_of(g, t) * LANES, (block_of(g, t) + 1) * LANES)
+                value = back[f, :, cols] - (omega * damp_in[g, t, 0:1]) * adv[f, :, cols]
+                for i, piece in enumerate(split_bf16(value)):
+                    split[
+                        i * bins_dev + f * ND : i * bins_dev + (f + 1) * ND, cols
+                    ] = piece
+    for j in range(cells // WIDE):
+        low, high = max(0, j * WIDE - land), min(sea_cells, (j + 1) * WIDE)
+        cols = slice(j * WIDE, (j + 1) * WIDE)
+        got = jnp.dot(
+            split[:, low:high], spread_ref[low:high, cols], preferred_element_type=f32
+        )
+        full_ref[:, cols] = got[:bins_dev] + got[bins_dev : 2 * bins_dev] + got[2 * bins_dev :]
+
+    block = held.at[0 : (group - 1) * freq_dev]
+    remote(block, block, y_sem, held_sem.at[0, 0], (me + 1) % count).wait_send()
+    remote(block, block, ret_send, ret_recv.at[0], (me + 1) % count).wait_send()
+    others = mom_in.at[0 : count - 1]
+    remote(others, others, mom_send, mom_recv, (me + 1) % count).wait_send()
+    others = damp_in.at[0 : group - 1]
+    remote(others, others, damp_send, damp_recv, (me + 1) % count).wait_send()
+    block = held.at[0:HALO]
+
+    @pl.when(zone < zones - 1)
+    def _():
+        remote(block, block, z_sem.at[0], halo_sem.at[0, 0], (me + 1) % count).wait_send()
+
+    @pl.when(zone > 0)
+    def _():
+        remote(block, block, z_sem.at[1], halo_sem.at[0, 0], (me + 1) % count).wait_send()
+
+    others = sum_in.at[0 : count - 1]
+    remote(others, others, sum_send, sum_recv, (me + 1) % count).wait()
     for g in range(group):
         mass = sum_in[g]
         for other in range(1, zones):
             mass = mass + sum_in[other * group + g]
-        height = 4.0 * jnp.sqrt(mass * (1.0 / (NF * ND)) + 1e-06)
         for t in range(parts):
-            height_ref[0:1, block_of(g, t) * LANES : (block_of(g, t) + 1) * LANES] = height[
-                :, t * LANES : (t + 1) * LANES
-            ]
-
-    for t in range(parts):
-        for i in range(1, group):
-            peer = rank_of(offsets[i])
-            remote(
-                done.at[pl.ds(0, freq_dev), :, lanes_of(t)], out_ref.at[:, :, tile_of(peer, t)],
-                ret_send.at[peer, t], ret_recv.at[peer, t], zone * group + peer,
-            ).wait_recv()
-            for f in range(freq_dev):
-                y_copy(f, i, t).wait_send()
-            ret_copy(peer, t).wait_send()
-    for step in range(1, count):
-        for t in range(parts):
-            remote(
-                mom_out.at[:, tile_of(0, t)], mom_in.at[me, :, lanes_of(t)],
-                mom_send.at[step - 1, t], mom_recv.at[me, t], (me + step) % count,
-            ).wait_send()
-        sum_copy(step).wait_send()
-
-    @pl.when(zone < zones - 1)
-    def _():
-        for t in range(parts):
-            for slot in range(freq_group - HALO, freq_group):
-                up_copy(slot, t).wait_send()
-
-    @pl.when(zone > 0)
-    def _():
-        for t in range(parts):
-            for slot in range(HALO):
-                down_copy(slot, t).wait_send()
+            mean = mass[:, t * LANES : (t + 1) * LANES] * (1.0 / (NF * ND)) - damp_in[g, t, 1:2]
+            cols = slice(block_of(g, t) * LANES, (block_of(g, t) + 1) * LANES)
+            height_ref[0:1, cols] = 4.0 * jnp.sqrt(mean + 1e-06)
 
 
 def store_kernel(
-    count, new_in, height_in, spread_in, new_out, wave_ref, mean_ref, split, full, tall, sem
+    count, full_in, height_in, spread_in, new_out, wave_ref, mean_ref, sem
 ):
-    rows, cells = full.shape
+    cells = full_in.shape[1]
     sea_cells = height_in.shape[1]
-    land = cells - sea_cells
-    f32 = jnp.float32
+    copy = pltpu.make_async_copy(full_in, new_out, sem)
+    copy.start()
     me = lax.axis_index("spec")
     height = height_in[...]
     mean_ref[...] = jnp.sum(height, axis=1, keepdims=True) * (1.0 / sea_cells)
-    for i, piece in enumerate(split_bf16(new_in[...].reshape(rows, sea_cells))):
-        split[i * rows : (i + 1) * rows, :] = piece
-    split[3 * rows :, :] = rows_of(split_bf16(height), split.shape[0] - 3 * rows, sea_cells)
-    copies = []
-    for j in range(cells // WIDE):
-        low, high = max(0, j * WIDE - land), min(sea_cells, (j + 1) * WIDE)
-        cols = slice(j * WIDE, (j + 1) * WIDE)
-        got = jnp.dot(
-            split[:, low:high], spread_in[low:high, cols], preferred_element_type=f32
-        )
-        full[:, cols] = got[:rows] + got[rows : 2 * rows] + got[2 * rows : 3 * rows]
-        tall[:, cols] = got[3 * rows : 3 * rows + 1] + got[3 * rows + 1 : 3 * rows + 2] + (
-            got[3 * rows + 2 : 3 * rows + 3]
-        )
-        copy = pltpu.make_async_copy(full.at[:, cols], new_out.at[:, cols], sem.at[j])
-        copy.start()
-        copies.append(copy)
     points = cells // count
-    row = LANES * points // math.gcd(LANES, points)
-    per_row = row // points
-    mine = tall[:, pl.ds(pl.multiple_of(me // per_row * row, LANES), row)]
-    shift = (me % per_row) * points
-    turned = pltpu.roll(jnp.broadcast_to(mine, (8, row)), (row - shift) % row, 1)
+    start = jnp.minimum(me * points // LANES * LANES, cells - WIDE)
+    window = spread_in[:, pl.ds(pl.multiple_of(start, LANES), WIDE)]
+    got = jnp.dot(
+        rows_of(split_bf16(height), ND // 2, sea_cells), window,
+        preferred_element_type=jnp.float32,
+    )
+    wave = got[0:1] + got[1:2] + got[2:3]
+    shift = me * points - start
+    turned = pltpu.roll(jnp.broadcast_to(wave, (8, WIDE)), (WIDE - shift) % WIDE, 1)
     wave_ref[...] = turned[0, :points]
-    for copy in copies:
-        copy.wait()
+    copy.wait()
 
 
 def fused_local(spectrum, sea_mask, wind_speed, wind_angle):
@@ -615,16 +621,14 @@
     width = sea_cells // group
     points = cells // count
     parts = width // LANES
-    blocks = sea_cells // LANES
-    reach = cells - sea_cells + LANES
-    tail = 16
+    reach = cells - sea_cells + WIDE
     f32, bf16 = jnp.float32, jnp.bfloat16
     dma = pltpu.SemaphoreType.DMA
     vmem = pl.BlockSpec(memory_space=pltpu.VMEM)
     handed = pl.pallas_call(
         functools.partial(fused_kernel, count, group),
         out_shape=(
-            pltpu.VMEM((freq_dev, ND, sea_cells), f32),
+            pltpu.VMEM((bins_dev, cells), f32),
             pltpu.VMEM((1, sea_cells), f32),
             pltpu.VMEM((sea_cells, cells), bf16),
         ),
@@ -638,31 +642,38 @@
             dma((3,)),
             pltpu.VMEM((bins_dev, cells), f32),
             pltpu.VMEM((bins_dev, cells), f32),
-            pltpu.VMEM((freq_dev, 3 * ND, cells), bf16),
-            pltpu.VMEM((blocks, reach, LANES), bf16),
+            pltpu.VMEM((3 * bins_dev, cells), bf16),
+            pltpu.VMEM((sea_cells // WIDE, reach, WIDE), bf16),
             pltpu.VMEM((ND // 2, cells), bf16),
             pltpu.VMEM((freq_dev, ND, sea_cells), f32),
             pltpu.VMEM((freq_group + 2 * HALO, ND, width), f32),
             pltpu.VMEM((freq_group, ND, width), f32),
-            pltpu.VMEM((2, sea_cells), f32),
-            pltpu.VMEM((count, 2, width), f32),
+            pltpu.VMEM((freq_dev, ND, sea_cells), f32),
+            pltpu.VMEM((parts, 2, group * LANES), f32),
+            pltpu.VMEM((count, parts, 2, LANES), f32),
             pltpu.VMEM((ND, width), f32),
             pltpu.VMEM((ND, width), f32),
             pltpu.VMEM((1, width), f32),
             pltpu.VMEM((count, 1, width), f32),
+            pltpu.VMEM((parts, 2, LANES), f32),
+            pltpu.VMEM((group, parts, 2, LANES), f32),
             dma((freq_dev,)),
             dma((freq_group + 2 * HALO, parts)),
-            dma((group - 1, freq_dev, parts)),
-            dma((HALO, parts)),
-            dma((HALO, parts)),
-            dma((count - 1, parts)),
-            dma((count, parts)),
-            dma((group, parts)),
-            dma((group, parts)),
-            dma((count - 1,)),
-            dma((count,)),
+            dma((2, parts)),
+            dma,
+            dma((2,)),
+            dma,
+            dma,
+            dma,
+            dma((parts,)),
+            dma,
+            dma,
+            dma,
+            dma,
         ],
-        compiler_params=pltpu.CompilerParams(collective_id=0, has_side_effects=True),
+        compiler_params=pltpu.CompilerParams(
+            collective_id=0, has_side_effects=True, vmem_limit_bytes=32 * 2**20
+        ),
     )(sea_mask, wind_speed, wind_angle, spectrum)
     out, wave, mean = pl.pallas_call(
         functools.partial(store_kernel, count),
@@ -673,12 +684,8 @@
         ),
         in_specs=[vmem] * 3,
         out_specs=(pl.BlockSpec(memory_space=pltpu.HBM), vmem, vmem),
-        scratch_shapes=[
-            pltpu.VMEM((3 * bins_dev + tail, sea_cells), bf16),
-            pltpu.VMEM((bins_dev, cells), f32),
-            pltpu.VMEM((1, cells), f32),
-            dma((cells // WIDE,)),
-        ],
+        scratch_shapes=[dma],
+        compiler_params=pltpu.CompilerParams(vmem_limit_bytes=16 * 2**20),
     )(*[pltpu.with_memory_space_constraint(piece, pltpu.VMEM) for piece in handed])
     return (out, wave, mean.reshape(1))
 

time: 26.3 us -> 26 us (0.989)
  Pallas kernels: 25.5 us -> 21.9 us
  local copies, waits for them, and re-layouts: 0 us -> 3.15 us
    unnamed x0 -> x8, local copies, waits for them, and re-layouts: none -> 3.15 us
    pallas_call x1, Pallas kernels: 23.6 us -> 20.5 us  [fused_local(): pl.pallas_call(functools.partial(fused_kernel, count, group), out_shape=(...]
    pallas_call x1, Pallas kernels: 1.9 us -> 1.35 us  [fused_local(): pl.pallas_call(functools.partial(store_kernel, count), out_shape=(pltpu.H...]
where the time goes in v1:
time: 26 us; the launch traced here: 25.7 us
  Pallas kernels  21.9 us (84%)
  local copies, waits for them, and re-layouts  3.15 us (12%)
  between operations  0.65 us (2%)
    pallas_call x1, Pallas kernels, fused_local(): pl.pallas_call(functools.partial(fused_kernel, count, group), out_shape=(...  20.5 us
    unnamed x8, local copies, waits for them, and re-layouts  3.15 us
    pallas_call x1, Pallas kernels, fused_local(): pl.pallas_call(functools.partial(store_kernel, count), out_shape=(pltpu.H...  1.35 us

profile of v1, /device:TPU:0, one launch (start us, length us, event | category | flops | bytes accessed | tf_op | source)
XLA Modules:
  0.0 25.7 jit_solution(15616159007200510929)
XLA Ops:
  0.6 0.0 copy-start
  0.6 1.1 %copy-done = f32[96,1536]{1,0:T(8,128)S(1)} copy-done((f32[96,1536]{1,0:T(8,128)S(1)}, f32[96,1536]{1,0:T(8,128)}, u32[]{:S(2)}) %copy-start) | copy-done | bytes 589848
  1.7 0.0 copy-start.1
  1.7 0.7 %copy-done.1 = s32[1536]{0:T(1024)S(1)} copy-done((s32[1536]{0:T(1024)S(1)}, s32[1536]{0:T(1024)}, u32[]{:S(2)}) %copy-start.1) | copy-done | bytes 6168
  2.4 0.0 copy-start.2
  2.4 0.7 %copy-done.2 = f32[1536]{0:T(1024)S(1)} copy-done((f32[1536]{0:T(1024)S(1)}, f32[1536]{0:T(1024)}, u32[]{:S(2)}) %copy-start.2) | copy-done | bytes 6168
  3.1 0.0 copy-start.3
  3.1 0.7 %copy-done.3 = f32[1536]{0:T(1024)S(1)} copy-done((f32[1536]{0:T(1024)S(1)}, f32[1536]{0:T(1024)}, u32[]{:S(2)}) %copy-start.3) | copy-done | bytes 6168
  3.8 20.5 %shard_map.67 = (f32[96,1536]{1,0:T(8,128)S(1)}, f32[1,1024]{1,0:T(1,128)S(1)}, bf16[1024,1536]{1,0:T(8,128)(2,1)S(1)}) custom-call(s32[1536]{0:T(1024)S(1)} %copy-done.1, f32[1536]{0:T(1024)S(1)} %copy-done.2, f32[1536]{0:T(1024)S(1)} %copy-done.3, f32[96,1536]{1,0:T(8,128)S(1)} %copy-done), custom_call_target="tpu_custom_call" | custom-call | tf_op jit(solution)/shard_map/pallas_call | solution.py:628
  24.3 1.4 %shard_map.68 = (f32[96,1536]{1,0:T(8,128)}, f32[96]{0:T(128)}, f32[1,1]{1,0:T(1,128)}) custom-call(f32[96,1536]{1,0:T(8,128)S(1)} %get-tuple-element.9.full_in, f32[1,1024]{1,0:T(1,128)S(1)} %get-tuple-element.10.height_in, bf16[1024,1536]{1,0:T(8,128)(2,1)S(1)} %get-tuple-element.11.spread_in), custom_call_target="tpu_custom_call" | custom-call | tf_op jit(solution)/shard_map/pallas_call | solution.py:678
Async XLA Ops:
  0.6 1.1 %copy-start = (f32[96,1536]{1,0:T(8,128)S(1)}, f32[96,1536]{1,0:T(8,128)}, u32[]{:S(2)}) copy-start(f32[96,1536]{1,0:T(8,128)} %spec_ref.1) | copy-start | bytes 1769476
  1.7 0.7 %copy-start.1 = (s32[1536]{0:T(1024)S(1)}, s32[1536]{0:T(1024)}, u32[]{:S(2)}) copy-start(s32[1536]{0:T(1024)} %sea_in.1) | copy-start | bytes 18436
  2.4 0.7 %copy-start.2 = (f32[1536]{0:T(1024)S(1)}, f32[1536]{0:T(1024)}, u32[]{:S(2)}) copy-start(f32[1536]{0:T(1024)} %wind_in.1) | copy-start | bytes 18436
  3.1 0.7 %copy-start.3 = (f32[1536]{0:T(1024)S(1)}, f32[1536]{0:T(1024)}, u32[]{:S(2)}) copy-start(f32[1536]{0:T(1024)} %angle_in.1) | copy-start | bytes 18436

commit v2 on v1

--- a/solution.py
+++ b/solution.py
@@ -162,9 +162,13 @@
     return out.astype(jnp.bfloat16)
 
 
+def window_start(count, me, cells):
+    return jnp.minimum(me * (cells // count) // LANES * LANES, cells - WIDE)
+
+
 def fused_kernel(
-    count, group, sea_in, wind_in, angle_in, spec_ref, full_ref, height_ref, spread_ref,
-    sea_raw, wind_raw, angle_raw, aux_ref, aux_sem,
+    count, group, sea_in, wind_in, angle_in, spec_ref, full_ref, height_ref, window_ref,
+    sea_raw, wind_raw, angle_raw, aux_ref, place_ref, spread_ref, aux_sem,
     raw, moved, split, pick, wsplit, adv, held, done, back, mom_out, mom_in, wind, acc,
     sum_out, sum_in, damp_out, damp_in,
     load_sem, held_sem, halo_sem, y_sem, z_sem, mom_send, mom_recv,
@@ -409,6 +413,12 @@
     places = [
         jnp.where(mask[i] > 0.0, ranks[i : i + 1] + before[i], LAND) for i in range(cell_tiles)
     ]
+    for i in range(cell_tiles):
+        place_ref[0:1, i * LANES : (i + 1) * LANES] = places[i]
+    start = window_start(count, me, cells)
+    mine = place_ref[0:1, pl.ds(pl.multiple_of(start, LANES), WIDE)]
+    sea_rows = lax.broadcasted_iota(jnp.int32, (sea_cells, WIDE), 0).astype(f32)
+    window_ref[...] = jnp.where(sea_rows == mine, 1.0, 0.0).astype(bf16)
     wide_rows = lax.broadcasted_iota(jnp.int32, (WIDE, LANES), 0).astype(f32)
     for u in range(sea_cells // WIDE):
         for i in range(cell_tiles):
@@ -588,7 +598,7 @@
 
 
 def store_kernel(
-    count, full_in, height_in, spread_in, new_out, wave_ref, mean_ref, sem
+    count, full_in, height_in, window_in, new_out, wave_ref, mean_ref, sem
 ):
     cells = full_in.shape[1]
     sea_cells = height_in.shape[1]
@@ -598,10 +608,9 @@
     height = height_in[...]
     mean_ref[...] = jnp.sum(height, axis=1, keepdims=True) * (1.0 / sea_cells)
     points = cells // count
-    start = jnp.minimum(me * points // LANES * LANES, cells - WIDE)
-    window = spread_in[:, pl.ds(pl.multiple_of(start, LANES), WIDE)]
+    start = window_start(count, me, cells)
     got = jnp.dot(
-        rows_of(split_bf16(height), ND // 2, sea_cells), window,
+        rows_of(split_bf16(height), ND // 2, sea_cells), window_in[...],
         preferred_element_type=jnp.float32,
     )
     wave = got[0:1] + got[1:2] + got[2:3]
@@ -630,7 +639,7 @@
         out_shape=(
             pltpu.VMEM((bins_dev, cells), f32),
             pltpu.VMEM((1, sea_cells), f32),
-            pltpu.VMEM((sea_cells, cells), bf16),
+            pltpu.VMEM((sea_cells, WIDE), bf16),
         ),
         in_specs=[pl.BlockSpec(memory_space=pl.ANY)] * 4,
         out_specs=(vmem,) * 3,
@@ -639,6 +648,8 @@
             pltpu.VMEM((cells,), f32),
             pltpu.VMEM((cells,), f32),
             pltpu.VMEM((1, cells), f32),
+            pltpu.VMEM((1, cells), f32),
+            pltpu.VMEM((sea_cells, cells), bf16),
             dma((3,)),
             pltpu.VMEM((bins_dev, cells), f32),
             pltpu.VMEM((bins_dev, cells), f32),
@@ -671,9 +682,7 @@
             dma,
             dma,
         ],
-        compiler_params=pltpu.CompilerParams(
-            collective_id=0, has_side_effects=True, vmem_limit_bytes=32 * 2**20
-        ),
+        compiler_params=pltpu.CompilerParams(collective_id=0, has_side_effects=True),
     )(sea_mask, wind_speed, wind_angle, spectrum)
     out, wave, mean = pl.pallas_call(
         functools.partial(store_kernel, count),
@@ -685,7 +694,6 @@
         in_specs=[vmem] * 3,
         out_specs=(pl.BlockSpec(memory_space=pltpu.HBM), vmem, vmem),
         scratch_shapes=[dma],
-        compiler_params=pltpu.CompilerParams(vmem_limit_bytes=16 * 2**20),
     )(*[pltpu.with_memory_space_constraint(piece, pltpu.VMEM) for piece in handed])
     return (out, wave, mean.reshape(1))
 

time: 26 us -> 22.4 us (0.86)
  local copies, waits for them, and re-layouts: 3.15 us -> 0 us
  Pallas kernels: 21.9 us -> 21.5 us
    unnamed x8 -> x0, local copies, waits for them, and re-layouts: 3.15 us -> none
    pallas_call x1, Pallas kernels: 20.5 us -> 20.1 us  [fused_local(): pl.pallas_call(functools.partial(fused_kernel, count, group), out_shape=(...]
where the time goes in v2:
time: 22.4 us; the launch traced here: 22.2 us
  Pallas kernels  21.5 us (96%)
  between operations  0.64 us (3%)
    pallas_call x1, Pallas kernels, fused_local(): pl.pallas_call(functools.partial(fused_kernel, count, group), out_shape=(...  20.1 us
    pallas_call x1, Pallas kernels, fused_local(): pl.pallas_call(functools.partial(store_kernel, count), out_shape=(pltpu.H...  1.4 us

profile of v2, /device:TPU:0, one launch (start us, length us, event | category | flops | bytes accessed | tf_op | source)
XLA Modules:
  0.0 22.2 jit_solution(3968887332398377315)
XLA Ops:
  0.6 20.1 %shard_map.67 = (f32[96,1536]{1,0:T(8,128)S(1)}, f32[1,1024]{1,0:T(1,128)S(1)}, bf16[1024,256]{1,0:T(8,128)(2,1)S(1)}) custom-call(s32[1536]{0:T(1024)} %sea_in.1, f32[1536]{0:T(1024)} %wind_in.1, f32[1536]{0:T(1024)} %angle_in.1, f32[96,1536]{1,0:T(8,128)} %spec_ref.1), custom_call_target="tpu_custom_call" | custom-call | tf_op jit(solution)/shard_map/pallas_call | solution.py:637
  20.8 1.4 %shard_map.68 = (f32[96,1536]{1,0:T(8,128)}, f32[96]{0:T(128)}, f32[1,1]{1,0:T(1,128)}) custom-call(f32[96,1536]{1,0:T(8,128)S(1)} %get-tuple-element.9.full_in, f32[1,1024]{1,0:T(1,128)S(1)} %get-tuple-element.10.height_in, bf16[1024,256]{1,0:T(8,128)(2,1)S(1)} %get-tuple-element.11.window_in), custom_call_target="tpu_custom_call" | custom-call | tf_op jit(solution)/shard_map/pallas_call | solution.py:687

commit v3 on v2

--- a/solution.py
+++ b/solution.py
@@ -169,9 +169,9 @@
 def fused_kernel(
     count, group, sea_in, wind_in, angle_in, spec_ref, full_ref, height_ref, window_ref,
     sea_raw, wind_raw, angle_raw, aux_ref, place_ref, spread_ref, aux_sem,
-    raw, moved, split, pick, wsplit, adv, held, done, back, mom_out, mom_in, wind, acc,
+    raw, moved, split, wsplit, adv, held, done, back, mom_out, mom_in, wind, acc,
     sum_out, sum_in, damp_out, damp_in,
-    load_sem, held_sem, halo_sem, y_sem, z_sem, mom_send, mom_recv,
+    load_sem, held_sem, halo_sem, y_sem, z_sem, chain_sem, mom_send, mom_recv,
     ret_send, ret_recv, sum_send, sum_recv, damp_send, damp_recv,
 ):
     f32, bf16 = jnp.float32, jnp.bfloat16
@@ -210,11 +210,22 @@
     for load in small[:1] + loads + small[1:]:
         load.start()
     barrier = pltpu.get_barrier_semaphore()
-    for step in range(1, count):
+
+    def signal(semaphore, target):
         pl.semaphore_signal(
-            barrier, inc=1, device_id={"spec": (me + step) % count},
-            device_id_type=pl.DeviceIdType.MESH,
-        )
+            semaphore, inc=1, device_id={"spec": target}, device_id_type=pl.DeviceIdType.MESH
+        )
+
+    for step in range(1, group):
+        signal(barrier, zone * group + (rank + step) % group)
+
+    @pl.when(zone > 0)
+    def _():
+        signal(barrier, me - group)
+
+    @pl.when(zone < zones - 1)
+    def _():
+        signal(barrier, me + group)
 
     @pl.when(zone == 0)
     def _():
@@ -238,12 +249,11 @@
     def rank_of(offset):
         return (side + offset[0]) % sides * 2 + (core + offset[1]) % 2
 
-    def y_copy(f, i, t):
-        peer = rank_of(offsets[i])
-        slot = HALO + rank * freq_dev + f
+    def y_copy(f, peer, t):
         return remote(
-            adv.at[f, :, tile_of(peer, t)], held.at[slot, :, lanes_of(t)],
-            y_sem, held_sem.at[slot, t], zone * group + peer,
+            adv.at[f, :, tile_of(peer, t)],
+            held.at[HALO + rank * freq_dev + f, :, lanes_of(t)],
+            y_sem, held_sem.at[rank, f, t], zone * group + peer,
         )
 
     dirs = lax.broadcasted_iota(jnp.int32, (ND, LANES), 0).astype(f32)
@@ -257,35 +267,37 @@
 
     square_rows = lax.broadcasted_iota(jnp.int32, (LANES, LANES), 0)
     square_cols = lax.broadcasted_iota(jnp.int32, (LANES, LANES), 1)
-    lane_ids = square_cols.astype(f32)
-    ones = jnp.ones((LANES, LANES), bf16)
-
     small[0].wait()
     aux_ref[...] = sea_raw[...].astype(f32).reshape(1, cells)
     sea = [aux_ref[0:1, r * NLON : (r + 1) * NLON] for r in range(lat_count)]
     mask = [aux_ref[0:1, i * LANES : (i + 1) * LANES] for i in range(cell_tiles)]
-    before = [jnp.zeros((1, 1), f32)]
+    tri_up = jnp.where(square_rows < square_cols, 1.0, 0.0).astype(bf16)
+    ranks = jnp.dot(rows_of(mask, ND // 2, LANES), tri_up, preferred_element_type=f32)
+    before = jnp.zeros((1, 1), f32)
     for i in range(cell_tiles):
-        before.append(before[i] + jnp.sum(mask[i], axis=1, keepdims=True))
-    for i in range(cell_tiles):
-        tri = jnp.where(
-            square_cols < square_rows,
-            mask[i],
-            jnp.where(square_cols == square_rows, LAND * (1.0 - mask[i]), 0.0),
-        )
-        within = jnp.dot(tri.astype(bf16), ones, preferred_element_type=f32)
-        place = within + before[i]
-        for p in range(sea_cells // WIDE):
-            row = i * LANES - p * WIDE
-            if 0 <= row < reach:
-                for h in range(WIDE // LANES):
-                    first = float(p * WIDE + h * LANES)
-                    hit = jnp.where(place == lane_ids + first, 1.0, 0.0)
-                    pick[p, row : row + LANES, h * LANES : (h + 1) * LANES] = hit.astype(bf16)
+        place_ref[0:1, i * LANES : (i + 1) * LANES] = jnp.where(
+            mask[i] > 0.0, ranks[i : i + 1] + before, LAND
+        )
+        before = before + jnp.sum(mask[i], axis=1, keepdims=True)
+    pair_rows = lax.broadcasted_iota(jnp.int32, (WIDE, reach), 0).astype(f32)
+
+    def build(pair):
+        cols = pl.ds(pl.multiple_of(pair * WIDE, LANES), reach)
+        first = (pair * WIDE).astype(f32)
+        hit = jnp.where(place_ref[0:1, cols] - first == pair_rows, 1.0, 0.0)
+        spread_ref[pl.ds(pl.multiple_of(pair * WIDE, LANES), WIDE), cols] = hit.astype(bf16)
+
+    def packed(values, pair):
+        cols = pl.ds(pl.multiple_of(pair * WIDE, LANES), reach)
+        return lax.dot_general(
+            values[:, cols],
+            spread_ref[pl.ds(pl.multiple_of(pair * WIDE, LANES), WIDE), cols],
+            (((1,), (1,)), ((), ())), preferred_element_type=f32,
+        )
 
     quarter = ND // 4
     tiles = NLON // LANES
-    for f in range(freq_dev):
+    def advect(f):
         loads[f].wait()
         freq = (me * freq_dev + f).astype(f32)
         speed = 0.2 * jnp.exp(jnp.full((quarter, LANES), -log_step, f32) * freq)
@@ -308,53 +320,139 @@
                 energy = fresh
             for r in range(lat_count):
                 moved[rows, r * NLON : (r + 1) * NLON] = energy[r]
-        rows = slice(f * ND, (f + 1) * ND)
-        for i, piece in enumerate(split_bf16(moved[rows])):
-            split[i * bins_dev + f * ND : i * bins_dev + (f + 1) * ND, :] = piece
-
-    pl.semaphore_wait(barrier, count - 1)
-
-    def packed(values, pair):
-        cols = pl.ds(pl.multiple_of(pair * WIDE, LANES), reach)
-        return jnp.dot(values[:, cols], pick[pair], preferred_element_type=f32)
-
-    for t in range(parts):
-        for dy in list(range(1, sides)) + [0]:
-            pair = t * sides + (side + dy) % sides
-            got = packed(split, pair)
-            got = got[:bins_dev] + got[bins_dev : 2 * bins_dev] + got[2 * bins_dev :]
-            cols = pl.ds(pl.multiple_of(pair * WIDE, LANES), WIDE)
-            mass, moment = None, None
-            for f in range(freq_dev):
-                piece = got[f * ND : (f + 1) * ND]
-                adv[f, :, cols] = piece
-                total = jnp.sum(piece, axis=0, keepdims=True)
-                scaled = omega_of(me * freq_dev + f, (1, WIDE)) * total
-                mass = total if f == 0 else mass + total
-                moment = scaled if f == 0 else moment + scaled
-            for f in range(freq_dev):
-                for dc in ((0, 1) if dy else (1,)):
-                    y_copy(f, dy * 2 + dc, t).start()
-            if dy == 0:
-                for f in range(freq_dev):
-                    held[HALO + rank * freq_dev + f, :, lanes_of(t)] = adv[
-                        f, :, tile_of(rank, t)
-                    ]
-            here = pl.ds(pl.multiple_of((side + dy) % sides * WIDE, LANES), WIDE)
-            mom_out[t, 0:1, here] = mass
-            mom_out[t, 1:2, here] = moment
+        for i, piece in enumerate(split_bf16(moved[f * ND : (f + 1) * ND])):
+            split[(3 * f + i) * ND : (3 * f + i + 1) * ND, :] = piece
 
     def cols_of(index):
         return pl.ds(pl.multiple_of(index * LANES, LANES), LANES)
 
-    for step in range(1, count):
-        target = (me + step) % count
-        remote(
-            mom_out.at[:, :, cols_of(target % group)], mom_in.at[me],
-            mom_send, mom_recv, target,
-        ).start()
-    mom_in[me] = mom_out[:, :, cols_of(rank)]
-
+    def side_of(dy):
+        return (side + dy) % sides
+
+    def pack(t, dy, begin, end):
+        pair = t * sides + side_of(dy)
+        got = packed(split.at[begin * 3 * ND : end * 3 * ND], pair)
+        cols = pl.ds(pl.multiple_of(pair * WIDE, LANES), WIDE)
+        here = pl.ds(pl.multiple_of(side_of(dy) * WIDE, LANES), WIDE)
+        mass, moment = None, None
+        for f in range(begin, end):
+            base = (f - begin) * 3 * ND
+            piece = got[base : base + ND] + got[base + ND : base + 2 * ND] + (
+                got[base + 2 * ND : base + 3 * ND]
+            )
+            adv[f, :, cols] = piece
+            total = jnp.sum(piece, axis=0, keepdims=True)
+            scaled = omega_of(me * freq_dev + f, (1, WIDE)) * total
+            mass = total if mass is None else mass + total
+            moment = scaled if moment is None else moment + scaled
+        if begin:
+            mass, moment = mass + mom_out[t, 0:1, here], moment + mom_out[t, 1:2, here]
+        mom_out[t, 0:1, here] = mass
+        mom_out[t, 1:2, here] = moment
+
+    def send_far(t, dy, begin, end):
+        for c in range(2):
+            for f in range(begin, end):
+                y_copy(f, side_of(dy) * 2 + c, t).start()
+
+    def up_copy(slot, t):
+        return remote(
+            held.at[HALO + slot, :, lanes_of(t)],
+            held.at[HALO + slot - freq_group, :, lanes_of(t)],
+            z_sem.at[0], halo_sem.at[0, t], (zone + 1) % zones * group + rank,
+        )
+
+    def down_copy(slot, t):
+        return remote(
+            held.at[HALO + slot, :, lanes_of(t)],
+            held.at[HALO + slot + freq_group, :, lanes_of(t)],
+            z_sem.at[1], halo_sem.at[1, t], (zone + zones - 1) % zones * group + rank,
+        )
+
+    def forward(slot, t):
+        @pl.when((slot >= freq_group - HALO) & (zone < zones - 1))
+        def _():
+            up_copy(slot, t).start()
+
+        @pl.when((slot < HALO) & (zone > 0))
+        def _():
+            down_copy(slot, t).start()
+
+    def send_near(t):
+        for f in range(freq_dev):
+            y_copy(f, rank_of((0, 1)), t).start()
+            held[HALO + rank * freq_dev + f, :, lanes_of(t)] = adv[f, :, tile_of(rank, t)]
+        for f in range(freq_dev):
+            forward(rank * freq_dev + f, t)
+
+    def arrive_group(dy, t):
+        for f in range(freq_dev):
+            for dc in range(2):
+                if (dy, dc) != (0, 0):
+                    source = rank_of((dy, dc))
+                    slot = source * freq_dev + f
+                    block = held.at[HALO + slot, :, lanes_of(t)]
+                    remote(
+                        block, block, y_sem, held_sem.at[source, f, t], (me + 1) % count
+                    ).wait_recv()
+                    forward(slot, t)
+
+    far = list(range(1, sides))
+    for dy in far:
+        build(side_of(dy))
+    advect(0)
+    for dy in far:
+        pack(0, dy, 0, 1)
+    advect(1)
+    pl.semaphore_wait(
+        barrier, group - 1 + jnp.where(zone > 0, 1, 0) + jnp.where(zone < zones - 1, 1, 0)
+    )
+    for dy in far:
+        send_far(0, dy, 0, 1)
+
+    @pl.when(zone == 0)
+    def _():
+        signal(chain_sem.at[0], (me + group) % count)
+
+    @pl.when(zone == zones - 1)
+    def _():
+        signal(chain_sem.at[1], (me + count - group) % count)
+
+    for f in range(2, freq_dev):
+        advect(f)
+    for dy in far:
+        pack(0, dy, 1, freq_dev)
+        send_far(0, dy, 1, freq_dev)
+    build(side)
+    pack(0, 0, 0, freq_dev)
+    send_near(0)
+    for t in range(1, parts):
+        for dy in far:
+            build(t * sides + side_of(dy))
+            pack(t, dy, 0, freq_dev)
+            send_far(t, dy, 0, freq_dev)
+        build(t * sides + side)
+        pack(t, 0, 0, freq_dev)
+        send_near(t)
+
+    def relay(level):
+        @pl.when(zone == level)
+        def _():
+            pl.semaphore_wait(chain_sem.at[0], 1)
+
+            @pl.when(zone < zones - 1)
+            def _():
+                signal(chain_sem.at[0], (me + group) % count)
+
+        @pl.when(zone == zones - 1 - level)
+        def _():
+            pl.semaphore_wait(chain_sem.at[1], 1)
+
+            @pl.when(zone > 0)
+            def _():
+                signal(chain_sem.at[1], (me + count - group) % count)
+
+    relay(1)
     small[1].wait()
     small[2].wait()
     speed_all = wind_raw[...].reshape(1, cells)
@@ -370,69 +468,22 @@
         across = own[3:4] + own[4:5] + own[5:6]
         wind[:, t * LANES : (t + 1) * LANES] = cos_h * along + sin_h * across
 
-    def up_copy(slot, t):
-        return remote(
-            held.at[HALO + slot, :, lanes_of(t)],
-            held.at[HALO + slot - freq_group, :, lanes_of(t)],
-            z_sem.at[0], halo_sem.at[0, t], (zone + 1) % zones * group + rank,
-        )
-
-    def down_copy(slot, t):
-        return remote(
-            held.at[HALO + slot, :, lanes_of(t)],
-            held.at[HALO + slot + freq_group, :, lanes_of(t)],
-            z_sem.at[1], halo_sem.at[1, t], (zone + zones - 1) % zones * group + rank,
-        )
-
-    def arrive(index, t):
-        block = held.at[index, :, lanes_of(t)]
-        remote(block, block, y_sem, held_sem.at[index, t], (me + 1) % count).wait_recv()
-
-    def arrive_group(dy, t):
-        for f in range(freq_dev):
-            for dc in range(2):
-                slot = rank_of((dy, dc)) * freq_dev + f
-                if (dy, dc) != (0, 0):
-                    arrive(HALO + slot, t)
-
-                @pl.when((slot >= freq_group - HALO) & (zone < zones - 1))
-                def _():
-                    up_copy(slot, t).start()
-
-                @pl.when((slot < HALO) & (zone > 0))
-                def _():
-                    down_copy(slot, t).start()
-
     for t in range(parts):
         arrive_group(0, t)
-
-    tri_up = jnp.where(square_rows < square_cols, 1.0, 0.0).astype(bf16)
-    ranks = jnp.dot(
-        rows_of(mask, 2 * quarter, LANES), tri_up, preferred_element_type=f32
-    )
-    places = [
-        jnp.where(mask[i] > 0.0, ranks[i : i + 1] + before[i], LAND) for i in range(cell_tiles)
-    ]
-    for i in range(cell_tiles):
-        place_ref[0:1, i * LANES : (i + 1) * LANES] = places[i]
+    for level in range(2, zones):
+        relay(level)
+    for step in range(1, count):
+        target = (me + step) % count
+        remote(
+            mom_out.at[:, :, cols_of(target % group)], mom_in.at[me],
+            mom_send, mom_recv, target,
+        ).start()
+    mom_in[me] = mom_out[:, :, cols_of(rank)]
     start = window_start(count, me, cells)
     mine = place_ref[0:1, pl.ds(pl.multiple_of(start, LANES), WIDE)]
     sea_rows = lax.broadcasted_iota(jnp.int32, (sea_cells, WIDE), 0).astype(f32)
     window_ref[...] = jnp.where(sea_rows == mine, 1.0, 0.0).astype(bf16)
-    wide_rows = lax.broadcasted_iota(jnp.int32, (WIDE, LANES), 0).astype(f32)
-    for u in range(sea_cells // WIDE):
-        for i in range(cell_tiles):
-            if u * WIDE < (i + 1) * LANES + LANES and (u + 1) * WIDE + LANES > i * LANES - land:
-                hit = jnp.where(wide_rows + float(u * WIDE) == places[i], 1.0, 0.0)
-                spread_ref[u * WIDE : (u + 1) * WIDE, i * LANES : (i + 1) * LANES] = hit.astype(
-                    bf16
-                )
-            else:
-                spread_ref[u * WIDE : (u + 1) * WIDE, i * LANES : (i + 1) * LANES] = jnp.zeros(
-                    (WIDE, LANES), bf16
-                )
-
-    for dy in range(1, sides):
+    for dy in far:
         arrive_group(dy, 0)
 
     acc[...] = jnp.zeros_like(acc)
@@ -557,19 +608,21 @@
                 cols = slice(block_of(g, t) * LANES, (block_of(g, t) + 1) * LANES)
                 value = back[f, :, cols] - (omega * damp_in[g, t, 0:1]) * adv[f, :, cols]
                 for i, piece in enumerate(split_bf16(value)):
-                    split[
-                        i * bins_dev + f * ND : i * bins_dev + (f + 1) * ND, cols
-                    ] = piece
+                    split[(3 * f + i) * ND : (3 * f + i + 1) * ND, cols] = piece
     for j in range(cells // WIDE):
         low, high = max(0, j * WIDE - land), min(sea_cells, (j + 1) * WIDE)
         cols = slice(j * WIDE, (j + 1) * WIDE)
         got = jnp.dot(
             split[:, low:high], spread_ref[low:high, cols], preferred_element_type=f32
         )
-        full_ref[:, cols] = got[:bins_dev] + got[bins_dev : 2 * bins_dev] + got[2 * bins_dev :]
+        for f in range(freq_dev):
+            base = 3 * f * ND
+            full_ref[f * ND : (f + 1) * ND, cols] = got[base : base + ND] + (
+                got[base + ND : base + 2 * ND]
+            ) + got[base + 2 * ND : base + 3 * ND]
 
     block = held.at[0 : (group - 1) * freq_dev]
-    remote(block, block, y_sem, held_sem.at[0, 0], (me + 1) % count).wait_send()
+    remote(block, block, y_sem, held_sem.at[0, 0, 0], (me + 1) % count).wait_send()
     remote(block, block, ret_send, ret_recv.at[0], (me + 1) % count).wait_send()
     others = mom_in.at[0 : count - 1]
     remote(others, others, mom_send, mom_recv, (me + 1) % count).wait_send()
@@ -630,7 +683,6 @@
     width = sea_cells // group
     points = cells // count
     parts = width // LANES
-    reach = cells - sea_cells + WIDE
     f32, bf16 = jnp.float32, jnp.bfloat16
     dma = pltpu.SemaphoreType.DMA
     vmem = pl.BlockSpec(memory_space=pltpu.VMEM)
@@ -654,7 +706,6 @@
             pltpu.VMEM((bins_dev, cells), f32),
             pltpu.VMEM((bins_dev, cells), f32),
             pltpu.VMEM((3 * bins_dev, cells), bf16),
-            pltpu.VMEM((sea_cells // WIDE, reach, WIDE), bf16),
             pltpu.VMEM((ND // 2, cells), bf16),
             pltpu.VMEM((freq_dev, ND, sea_cells), f32),
             pltpu.VMEM((freq_group + 2 * HALO, ND, width), f32),
@@ -669,10 +720,11 @@
             pltpu.VMEM((parts, 2, LANES), f32),
             pltpu.VMEM((group, parts, 2, LANES), f32),
             dma((freq_dev,)),
-            dma((freq_group + 2 * HALO, parts)),
+            dma((group, freq_dev, parts)),
             dma((2, parts)),
             dma,
             dma((2,)),
+            pltpu.SemaphoreType.REGULAR((2,)),
             dma,
             dma,
             dma,

time: 22.4 us -> 21.8 us (0.973)
  Pallas kernels: 21.5 us -> 20.9 us
    pallas_call x1, Pallas kernels: 20.1 us -> 19.5 us  [fused_local(): pl.pallas_call(functools.partial(fused_kernel, count, group), out_shape=(...]
where the time goes in v3:
time: 21.8 us; the launch traced here: 21.6 us
  Pallas kernels  20.9 us (96%)
  between operations  0.64 us (3%)
    pallas_call x1, Pallas kernels, fused_local(): pl.pallas_call(functools.partial(fused_kernel, count, group), out_shape=(...  19.5 us
    pallas_call x1, Pallas kernels, fused_local(): pl.pallas_call(functools.partial(store_kernel, count), out_shape=(pltpu.H...  1.4 us

profile of v3, /device:TPU:0, one launch (start us, length us, event | category | flops | bytes accessed | tf_op | source)
XLA Modules:
  0.0 21.6 jit_solution(1534257041051304992)
XLA Ops:
  0.6 19.5 %shard_map.67 = (f32[96,1536]{1,0:T(8,128)S(1)}, f32[1,1024]{1,0:T(1,128)S(1)}, bf16[1024,256]{1,0:T(8,128)(2,1)S(1)}) custom-call(s32[1536]{0:T(1024)} %sea_in.1, f32[1536]{0:T(1024)} %wind_in.1, f32[1536]{0:T(1024)} %angle_in.1, f32[96,1536]{1,0:T(8,128)} %spec_ref.1), custom_call_target="tpu_custom_call" | custom-call | tf_op jit(solution)/shard_map/pallas_call | solution.py:689
  20.2 1.4 %shard_map.68 = (f32[96,1536]{1,0:T(8,128)}, f32[96]{0:T(128)}, f32[1,1]{1,0:T(1,128)}) custom-call(f32[96,1536]{1,0:T(8,128)S(1)} %get-tuple-element.9.full_in, f32[1,1024]{1,0:T(1,128)S(1)} %get-tuple-element.10.height_in, bf16[1024,256]{1,0:T(8,128)(2,1)S(1)} %get-tuple-element.11.window_in), custom_call_target="tpu_custom_call" | custom-call | tf_op jit(solution)/shard_map/pallas_call | solution.py:739

commit v4 on v3

--- a/solution.py
+++ b/solution.py
@@ -167,7 +167,7 @@
 
 
 def fused_kernel(
-    count, group, sea_in, wind_in, angle_in, spec_ref, full_ref, height_ref, window_ref,
+    count, group, sea_in, wind_in, angle_in, spec_ref, full_ref, height_ref, near_ref,
     sea_raw, wind_raw, angle_raw, aux_ref, place_ref, spread_ref, aux_sem,
     raw, moved, split, wsplit, adv, held, done, back, mom_out, mom_in, wind, acc,
     sum_out, sum_in, damp_out, damp_in,
@@ -221,11 +221,13 @@
 
     @pl.when(zone > 0)
     def _():
-        signal(barrier, me - group)
+        for c in range(2):
+            signal(barrier, (zone - 1) * group + side * 2 + c)
 
     @pl.when(zone < zones - 1)
     def _():
-        signal(barrier, me + group)
+        for c in range(2):
+            signal(barrier, (zone + 1) * group + side * 2 + c)
 
     @pl.when(zone == 0)
     def _():
@@ -369,21 +371,53 @@
             z_sem.at[1], halo_sem.at[1, t], (zone + zones - 1) % zones * group + rank,
         )
 
+    def early_up(f, c, t):
+        slot = rank * freq_dev + f
+        return remote(
+            adv.at[f, :, tile_of(side * 2 + c, t)],
+            held.at[HALO + slot - freq_group, :, lanes_of(t)],
+            z_sem.at[0], halo_sem.at[0, t], (zone + 1) % zones * group + side * 2 + c,
+        )
+
+    def early_down(f, c, t):
+        slot = rank * freq_dev + f
+        return remote(
+            adv.at[f, :, tile_of(side * 2 + c, t)],
+            held.at[HALO + slot + freq_group, :, lanes_of(t)],
+            z_sem.at[1], halo_sem.at[1, t], (zone + zones - 1) % zones * group + side * 2 + c,
+        )
+
+    def goes_up(slot):
+        return (slot >= freq_group - HALO) & (zone < zones - 1)
+
+    def goes_down(slot):
+        return (slot < HALO) & (zone > 0)
+
     def forward(slot, t):
-        @pl.when((slot >= freq_group - HALO) & (zone < zones - 1))
+        @pl.when(goes_up(slot))
         def _():
             up_copy(slot, t).start()
 
-        @pl.when((slot < HALO) & (zone > 0))
+        @pl.when(goes_down(slot))
         def _():
             down_copy(slot, t).start()
 
     def send_near(t):
         for f in range(freq_dev):
             y_copy(f, rank_of((0, 1)), t).start()
+        for f in range(freq_dev):
+            @pl.when(goes_up(rank * freq_dev + f))
+            def _():
+                for c in range(2):
+                    early_up(f, c, t).start()
+
+            @pl.when(goes_down(rank * freq_dev + f))
+            def _():
+                for c in range(2):
+                    early_down(f, c, t).start()
+
+        for f in range(freq_dev):
             held[HALO + rank * freq_dev + f, :, lanes_of(t)] = adv[f, :, tile_of(rank, t)]
-        for f in range(freq_dev):
-            forward(rank * freq_dev + f, t)
 
     def arrive_group(dy, t):
         for f in range(freq_dev):
@@ -395,7 +429,8 @@
                     remote(
                         block, block, y_sem, held_sem.at[source, f, t], (me + 1) % count
                     ).wait_recv()
-                    forward(slot, t)
+                    if dy:
+                        forward(slot, t)
 
     far = list(range(1, sides))
     for dy in far:
@@ -405,7 +440,7 @@
         pack(0, dy, 0, 1)
     advect(1)
     pl.semaphore_wait(
-        barrier, group - 1 + jnp.where(zone > 0, 1, 0) + jnp.where(zone < zones - 1, 1, 0)
+        barrier, group - 1 + jnp.where(zone > 0, 2, 0) + jnp.where(zone < zones - 1, 2, 0)
     )
     for dy in far:
         send_far(0, dy, 0, 1)
@@ -480,9 +515,7 @@
         ).start()
     mom_in[me] = mom_out[:, :, cols_of(rank)]
     start = window_start(count, me, cells)
-    mine = place_ref[0:1, pl.ds(pl.multiple_of(start, LANES), WIDE)]
-    sea_rows = lax.broadcasted_iota(jnp.int32, (sea_cells, WIDE), 0).astype(f32)
-    window_ref[...] = jnp.where(sea_rows == mine, 1.0, 0.0).astype(bf16)
+    near_ref[...] = place_ref[0:1, pl.ds(pl.multiple_of(start, LANES), WIDE)]
     for dy in far:
         arrive_group(dy, 0)
 
@@ -586,8 +619,6 @@
         for dy in range(1, sides):
             arrive_group(dy, t)
         first_half(t)
-        if t == parts - 1:
-            damping_terms()
         second_half(t - 1)
     second_half(parts - 1)
 
@@ -595,6 +626,7 @@
     for step in range(1, count):
         remote(sum_out, sum_in.at[me], sum_send, sum_recv, (me + step) % count).start()
     sum_in[me] = sum_out[...]
+    damping_terms()
 
     others = damp_in.at[0 : group - 1]
     remote(others, others, damp_send, damp_recv, (me + 1) % count).wait_recv()
@@ -628,15 +660,33 @@
     remote(others, others, mom_send, mom_recv, (me + 1) % count).wait_send()
     others = damp_in.at[0 : group - 1]
     remote(others, others, damp_send, damp_recv, (me + 1) % count).wait_send()
-    block = held.at[0:HALO]
-
-    @pl.when(zone < zones - 1)
-    def _():
-        remote(block, block, z_sem.at[0], halo_sem.at[0, 0], (me + 1) % count).wait_send()
-
-    @pl.when(zone > 0)
-    def _():
-        remote(block, block, z_sem.at[1], halo_sem.at[0, 0], (me + 1) % count).wait_send()
+    def drain(slots, way):
+        block = held.at[0:slots]
+        remote(
+            block, block, z_sem.at[way], halo_sem.at[0, 0], (me + 1) % count
+        ).wait_send()
+
+    for f in range(freq_dev):
+        @pl.when(goes_up(rank * freq_dev + f))
+        def _():
+            drain(2, 0)
+
+        @pl.when(goes_down(rank * freq_dev + f))
+        def _():
+            drain(2, 1)
+
+    for dy in far:
+        for c in range(2):
+            for f in range(freq_dev):
+                slot = (side_of(dy) * 2 + c) * freq_dev + f
+
+                @pl.when(goes_up(slot))
+                def _():
+                    drain(1, 0)
+
+                @pl.when(goes_down(slot))
+                def _():
+                    drain(1, 1)
 
     others = sum_in.at[0 : count - 1]
     remote(others, others, sum_send, sum_recv, (me + 1) % count).wait()
@@ -651,26 +701,36 @@
 
 
 def store_kernel(
-    count, full_in, height_in, window_in, new_out, wave_ref, mean_ref, sem
+    count, full_in, height_in, near_in, new_out, wave_out, mean_out, wave_ref, mean_ref, sem
 ):
     cells = full_in.shape[1]
     sea_cells = height_in.shape[1]
-    copy = pltpu.make_async_copy(full_in, new_out, sem)
-    copy.start()
+    copies = [
+        pltpu.make_async_copy(full_in, new_out, sem.at[0]),
+        pltpu.make_async_copy(wave_ref, wave_out, sem.at[1]),
+        pltpu.make_async_copy(mean_ref, mean_out, sem.at[2]),
+    ]
+    copies[0].start()
     me = lax.axis_index("spec")
-    height = height_in[...]
-    mean_ref[...] = jnp.sum(height, axis=1, keepdims=True) * (1.0 / sea_cells)
     points = cells // count
-    start = window_start(count, me, cells)
-    got = jnp.dot(
-        rows_of(split_bf16(height), ND // 2, sea_cells), window_in[...],
-        preferred_element_type=jnp.float32,
-    )
-    wave = got[0:1] + got[1:2] + got[2:3]
-    shift = me * points - start
-    turned = pltpu.roll(jnp.broadcast_to(wave, (8, WIDE)), (WIDE - shift) % WIDE, 1)
-    wave_ref[...] = turned[0, :points]
-    copy.wait()
+    shift = me * points - window_start(count, me, cells)
+    halves = []
+    for h in range(WIDE // LANES):
+        place = jnp.broadcast_to(near_in[:, h * LANES : (h + 1) * LANES], (8, LANES))
+        place = place.astype(jnp.int32)
+        wave = jnp.zeros((8, LANES), jnp.float32)
+        for b in range(sea_cells // LANES):
+            values = jnp.broadcast_to(height_in[:, b * LANES : (b + 1) * LANES], (8, LANES))
+            found = jnp.take_along_axis(values, place % LANES, axis=1)
+            wave = jnp.where(place // LANES == b, found, wave)
+        halves.append(wave)
+    wave = jnp.concatenate(halves, axis=1)
+    wave_ref[...] = pltpu.roll(wave, (WIDE - shift) % WIDE, 1)[0, :points]
+    copies[1].start()
+    mean_ref[...] = jnp.sum(height_in[...], axis=1, keepdims=True) * (1.0 / sea_cells)
+    copies[2].start()
+    for copy in copies:
+        copy.wait()
 
 
 def fused_local(spectrum, sea_mask, wind_speed, wind_angle):
@@ -691,7 +751,7 @@
         out_shape=(
             pltpu.VMEM((bins_dev, cells), f32),
             pltpu.VMEM((1, sea_cells), f32),
-            pltpu.VMEM((sea_cells, WIDE), bf16),
+            pltpu.VMEM((1, WIDE), f32),
         ),
         in_specs=[pl.BlockSpec(memory_space=pl.ANY)] * 4,
         out_specs=(vmem,) * 3,
@@ -740,12 +800,12 @@
         functools.partial(store_kernel, count),
         out_shape=(
             pltpu.HBM((bins_dev, cells), f32),
-            jax.ShapeDtypeStruct((points,), f32),
-            jax.ShapeDtypeStruct((1, 1), f32),
+            pltpu.HBM((points,), f32),
+            pltpu.HBM((1, 1), f32),
         ),
         in_specs=[vmem] * 3,
-        out_specs=(pl.BlockSpec(memory_space=pltpu.HBM), vmem, vmem),
-        scratch_shapes=[dma],
+        out_specs=(pl.BlockSpec(memory_space=pltpu.HBM),) * 3,
+        scratch_shapes=[pltpu.VMEM((points,), f32), pltpu.VMEM((1, 1), f32), dma((3,))],
     )(*[pltpu.with_memory_space_constraint(piece, pltpu.VMEM) for piece in handed])
     return (out, wave, mean.reshape(1))
 

time: 21.8 us -> 21.1 us (0.968)
  Pallas kernels: 20.9 us -> 20.2 us
    pallas_call x1, Pallas kernels: 1.4 us -> 0.85 us  [fused_local(): pl.pallas_call(functools.partial(store_kernel, count), out_shape=(pltpu.H...]
where the time goes in v4:
time: 21.1 us; the launch traced here: 20.9 us
  Pallas kernels  20.2 us (96%)
  between operations  0.64 us (3%)
    pallas_call x1, Pallas kernels, fused_local(): pl.pallas_call(functools.partial(fused_kernel, count, group), out_shape=(...  19.4 us
    pallas_call x1, Pallas kernels, fused_local(): pl.pallas_call(functools.partial(store_kernel, count), out_shape=(pltpu.H...  0.85 us

profile of v4, /device:TPU:0, one launch (start us, length us, event | category | flops | bytes accessed | tf_op | source)
XLA Modules:
  0.0 20.9 jit_solution(9165621211267026263)
XLA Ops:
  0.6 19.4 %shard_map.67 = (f32[96,1536]{1,0:T(8,128)S(1)}, f32[1,1024]{1,0:T(1,128)S(1)}, f32[1,256]{1,0:T(1,128)S(1)}) custom-call(s32[1536]{0:T(1024)} %sea_in.1, f32[1536]{0:T(1024)} %wind_in.1, f32[1536]{0:T(1024)} %angle_in.1, f32[96,1536]{1,0:T(8,128)} %spec_ref.1), custom_call_target="tpu_custom_call" | custom-call | tf_op jit(solution)/shard_map/pallas_call | solution.py:749
  20.0 0.9 %shard_map.68 = (f32[96,1536]{1,0:T(8,128)}, f32[96]{0:T(128)}, f32[1,1]{1,0:T(1,128)}) custom-call(f32[96,1536]{1,0:T(8,128)S(1)} %get-tuple-element.9.full_in, f32[1,1024]{1,0:T(1,128)S(1)} %get-tuple-element.10.height_in, f32[1,256]{1,0:T(1,128)S(1)} %get-tuple-element.11.near_in), custom_call_target="tpu_custom_call" | custom-call | tf_op jit(solution)/shard_map/pallas_call | solution.py:799

commit v5 on v4

--- a/solution.py
+++ b/solution.py
@@ -403,24 +403,23 @@
             down_copy(slot, t).start()
 
     def send_near(t):
+        for c in range(2):
+            for f in range(freq_dev):
+                @pl.when(goes_up(rank * freq_dev + f))
+                def _():
+                    early_up(f, c, t).start()
+
+                @pl.when(goes_down(rank * freq_dev + f))
+                def _():
+                    early_down(f, c, t).start()
+
         for f in range(freq_dev):
             y_copy(f, rank_of((0, 1)), t).start()
         for f in range(freq_dev):
-            @pl.when(goes_up(rank * freq_dev + f))
-            def _():
-                for c in range(2):
-                    early_up(f, c, t).start()
-
-            @pl.when(goes_down(rank * freq_dev + f))
-            def _():
-                for c in range(2):
-                    early_down(f, c, t).start()
-
-        for f in range(freq_dev):
             held[HALO + rank * freq_dev + f, :, lanes_of(t)] = adv[f, :, tile_of(rank, t)]
 
-    def arrive_group(dy, t):
-        for f in range(freq_dev):
+    def arrive_group(dy, t, begin, end):
+        for f in range(begin, end):
             for dc in range(2):
                 if (dy, dc) != (0, 0):
                     source = rank_of((dy, dc))
@@ -431,6 +430,28 @@
                     ).wait_recv()
                     if dy:
                         forward(slot, t)
+
+    def up_relay(level):
+        @pl.when(zone == level)
+        def _():
+            pl.semaphore_wait(chain_sem.at[0], 1)
+            if level < zones - 1:
+                signal(chain_sem.at[0], (me + group) % count)
+
+    def down_relay(level):
+        @pl.when(zone == level)
+        def _():
+            pl.semaphore_wait(chain_sem.at[1], 1)
+            if level > 0:
+                signal(chain_sem.at[1], (me + count - group) % count)
+
+    def send_moments():
+        for step in range(1, count):
+            target = (me + step) % count
+            remote(
+                mom_out.at[:, :, cols_of(target % group)], mom_in.at[me],
+                mom_send, mom_recv, target,
+            ).start()
 
     far = list(range(1, sides))
     for dy in far:
@@ -453,11 +474,14 @@
     def _():
         signal(chain_sem.at[1], (me + count - group) % count)
 
+    up_relay(1)
     for f in range(2, freq_dev):
         advect(f)
     for dy in far:
         pack(0, dy, 1, freq_dev)
         send_far(0, dy, 1, freq_dev)
+    for level in range(2, zones - 1):
+        up_relay(level)
     build(side)
     pack(0, 0, 0, freq_dev)
     send_near(0)
@@ -470,24 +494,22 @@
         pack(t, 0, 0, freq_dev)
         send_near(t)
 
-    def relay(level):
-        @pl.when(zone == level)
-        def _():
-            pl.semaphore_wait(chain_sem.at[0], 1)
-
-            @pl.when(zone < zones - 1)
-            def _():
-                signal(chain_sem.at[0], (me + group) % count)
-
-        @pl.when(zone == zones - 1 - level)
-        def _():
-            pl.semaphore_wait(chain_sem.at[1], 1)
-
-            @pl.when(zone > 0)
-            def _():
-                signal(chain_sem.at[1], (me + count - group) % count)
-
-    relay(1)
+    up_relay(zones - 1)
+    down_relay(zones - 2)
+
+    @pl.when(zone >= zones // 2)
+    def _():
+        send_moments()
+
+    for dy in far:
+        arrive_group(dy, 0, 0, 1)
+    for level in range(zones - 3, 0, -1):
+        down_relay(level)
+
+    @pl.when((zone < zones // 2) & (zone > 0))
+    def _():
+        send_moments()
+
     small[1].wait()
     small[2].wait()
     speed_all = wind_raw[...].reshape(1, cells)
@@ -503,21 +525,19 @@
         across = own[3:4] + own[4:5] + own[5:6]
         wind[:, t * LANES : (t + 1) * LANES] = cos_h * along + sin_h * across
 
-    for t in range(parts):
-        arrive_group(0, t)
-    for level in range(2, zones):
-        relay(level)
-    for step in range(1, count):
-        target = (me + step) % count
-        remote(
-            mom_out.at[:, :, cols_of(target % group)], mom_in.at[me],
-            mom_send, mom_recv, target,
-        ).start()
+    for dy in far:
+        arrive_group(dy, 0, 1, freq_dev)
+    down_relay(0)
+
+    @pl.when(zone == 0)
+    def _():
+        send_moments()
+
     mom_in[me] = mom_out[:, :, cols_of(rank)]
     start = window_start(count, me, cells)
     near_ref[...] = place_ref[0:1, pl.ds(pl.multiple_of(start, LANES), WIDE)]
-    for dy in far:
-        arrive_group(dy, 0)
+    for t in range(parts):
+        arrive_group(0, t, 0, freq_dev)
 
     acc[...] = jnp.zeros_like(acc)
     ascending = side > 0
@@ -539,42 +559,64 @@
             ret_send, ret_recv.at[t], zone * group + owner,
         )
 
+    def turn(values, amount):
+        return pltpu.roll(values, amount % ND, 0)
+
+    def rate(a, p, m):
+        return a * (a * (p + m) - 2.0 * (p * m))
+
+    def scale(index, factor):
+        return jnp.where((index >= 3) & (index <= NF - 3), factor, 0.0).astype(f32)
+
+    def slab(k, t):
+        return held[HALO + k, :, t * LANES : (t + 1) * LANES]
+
+    def rates(own, p2, m3):
+        return rate(own, turn(p2, -1), turn(m3, 3)) + rate(own, turn(p2, 1), turn(m3, -3))
+
+    def grown(own, freq, t):
+        omega = omega_of(freq, (1, LANES))
+        push = wind[:, t * LANES : (t + 1) * LANES] * omega - 1.0
+        return own + (0.05 * omega) * jnp.maximum(0.0, push) * own
+
+    def tally(energy, near, freq, t):
+        flow = scale(freq, 0.001) * near
+        acc[:, t * LANES : (t + 1) * LANES] += energy + (flow + flow - 2.0 * flow)
+
     def sources(t, begin, end):
-        lanes = slice(t * LANES, (t + 1) * LANES)
-
         def source_step(i, carry):
             k = jnp.where(ascending, i, freq_group - 1 - i)
             freq = zone * freq_group + k
-
-            def scale(index, factor):
-                return jnp.where((index >= 3) & (index <= NF - 3), factor, 0.0).astype(f32)
-
-            w_own = scale(freq, -0.002)
-            w_low, w_high = scale(freq - 2, 0.001), scale(freq + 3, 0.001)
-            omega = omega_of(freq, (1, LANES))
-
-            def slab(shift):
-                return held[HALO + k + shift, :, lanes]
-
-            def turn(values, amount):
-                return pltpu.roll(values, amount % ND, 0)
-
-            def rate(a, p, m):
-                return a * (a * (p + m) - 2.0 * (p * m))
-
-            own = slab(0)
-            p2, m3, m2, m5, p3, p5 = (slab(shift) for shift in (2, -3, -2, -5, 3, 5))
-            near = rate(own, turn(p2, -1), turn(m3, 3)) + rate(own, turn(p2, 1), turn(m3, -3))
+            own = slab(k, t)
+            p2, m3, m2, m5, p3, p5 = (slab(k + shift, t) for shift in (2, -3, -2, -5, 3, 5))
+            near = rates(own, p2, m3)
             low = rate(turn(m2, 1), own, turn(m5, 4)) + rate(turn(m2, -1), own, turn(m5, -4))
             high = rate(turn(p3, -3), turn(p5, -4), own) + rate(turn(p3, 3), turn(p5, 4), own)
-            interaction = w_own * near + w_low * low + w_high * high
-            gain = (0.05 * omega) * jnp.maximum(0.0, wind[:, lanes] * omega - 1.0)
-            fresh = own + gain * own + interaction
-            done[k, :, lanes] = fresh
-            acc[:, lanes] += fresh
+            interaction = scale(freq, -0.002) * near + scale(freq - 2, 0.001) * low + (
+                scale(freq + 3, 0.001) * high
+            )
+            energy = grown(own, freq, t)
+            done[k, :, t * LANES : (t + 1) * LANES] = energy + interaction
+            if begin == 0:
+                tally(energy, near, freq, t)
             return carry
 
         lax.fori_loop(begin, end, source_step, 0)
+
+    def tally_rest(t):
+        def rest_step(i, carry):
+            k = jnp.where(ascending, half + i, half - 1 - i)
+            center = jnp.where(
+                ascending,
+                jnp.where(i < 2, i - 2, half + i - 2),
+                jnp.where(i < 3, freq_group + i, half + 2 - i),
+            )
+            near = rates(slab(center, t), slab(center + 2, t), slab(center - 3, t))
+            energy = grown(slab(k, t), zone * freq_group + k, t)
+            tally(energy, near, zone * freq_group + center, t)
+            return carry
+
+        lax.fori_loop(0, half, rest_step, 0)
 
     half = freq_group // 2
     near_side = rank_of((0, 1))
@@ -582,11 +624,24 @@
     def first_half(t):
         arrive_halo(jnp.logical_not(ascending), t)
         sources(t, 0, half)
+        if t == parts - 1:
+            tally_rest(t)
+            send_sums()
         for dy in range(1, sides):
             for dc in range(2):
                 ret_copy(rank_of((dy, dc)), t).start()
+        if t < parts - 1:
+            tally_rest(t)
+
+    def send_sums():
+        sum_out[...] = jnp.sum(acc[...], axis=0, keepdims=True)
+        for step in range(1, count):
+            remote(sum_out, sum_in.at[me], sum_send, sum_recv, (me + step) % count).start()
+        sum_in[me] = sum_out[...]
 
     def second_half(t):
+        if t == parts - 1:
+            damping_terms()
         arrive_halo(ascending, t)
         sources(t, half, freq_group)
         ret_copy(near_side, t).start()
@@ -617,16 +672,10 @@
     first_half(0)
     for t in range(1, parts):
         for dy in range(1, sides):
-            arrive_group(dy, t)
+            arrive_group(dy, t, 0, freq_dev)
         first_half(t)
         second_half(t - 1)
     second_half(parts - 1)
-
-    sum_out[...] = jnp.sum(acc[...], axis=0, keepdims=True)
-    for step in range(1, count):
-        remote(sum_out, sum_in.at[me], sum_send, sum_recv, (me + step) % count).start()
-    sum_in[me] = sum_out[...]
-    damping_terms()
 
     others = damp_in.at[0 : group - 1]
     remote(others, others, damp_send, damp_recv, (me + 1) % count).wait_recv()

time: 21.1 us -> 18.7 us (0.89)
  Pallas kernels: 20.2 us -> 17.9 us
    pallas_call x1, Pallas kernels: 19.4 us -> 17 us  [fused_local(): pl.pallas_call(functools.partial(fused_kernel, count, group), out_shape=(...]
where the time goes in v5:
time: 18.7 us; the launch traced here: 18.5 us
  Pallas kernels  17.9 us (96%)
  between operations  0.64 us (3%)
    pallas_call x1, Pallas kernels, fused_local(): pl.pallas_call(functools.partial(fused_kernel, count, group), out_shape=(...  17 us
    pallas_call x1, Pallas kernels, fused_local(): pl.pallas_call(functools.partial(store_kernel, count), out_shape=(pltpu.H...  0.85 us

profile of v5, /device:TPU:0, one launch (start us, length us, event | category | flops | bytes accessed | tf_op | source)
XLA Modules:
  0.0 18.5 jit_solution(3533639850468453917)
XLA Ops:
  0.6 17.0 %shard_map.67 = (f32[96,1536]{1,0:T(8,128)S(1)}, f32[1,1024]{1,0:T(1,128)S(1)}, f32[1,256]{1,0:T(1,128)S(1)}) custom-call(s32[1536]{0:T(1024)} %sea_in.1, f32[1536]{0:T(1024)} %wind_in.1, f32[1536]{0:T(1024)} %angle_in.1, f32[96,1536]{1,0:T(8,128)} %spec_ref.1), custom_call_target="tpu_custom_call" | custom-call | tf_op jit(solution)/shard_map/pallas_call | solution.py:798
  17.7 0.9 %shard_map.68 = (f32[96,1536]{1,0:T(8,128)}, f32[96]{0:T(128)}, f32[1,1]{1,0:T(1,128)}) custom-call(f32[96,1536]{1,0:T(8,128)S(1)} %get-tuple-element.9.full_in, f32[1,1024]{1,0:T(1,128)S(1)} %get-tuple-element.10.height_in, f32[1,256]{1,0:T(1,128)S(1)} %get-tuple-element.11.near_in), custom_call_target="tpu_custom_call" | custom-call | tf_op jit(solution)/shard_map/pallas_call | solution.py:848

commit v6 on v5

--- a/solution.py
+++ b/solution.py
@@ -287,7 +287,9 @@
         cols = pl.ds(pl.multiple_of(pair * WIDE, LANES), reach)
         first = (pair * WIDE).astype(f32)
         hit = jnp.where(place_ref[0:1, cols] - first == pair_rows, 1.0, 0.0)
-        spread_ref[pl.ds(pl.multiple_of(pair * WIDE, LANES), WIDE), cols] = hit.astype(bf16)
+        spread_ref[pl.ds(pl.multiple_of(pair * WIDE, LANES), WIDE), cols] = hit.astype(
+            spread_ref.dtype
+        )
 
     def packed(values, pair):
         cols = pl.ds(pl.multiple_of(pair * WIDE, LANES), reach)
@@ -310,15 +312,18 @@
             cx0 = speed * jnp.abs(cos_h[part])
             cy = jnp.concatenate([speed * jnp.abs(sin_h[part])] * tiles, axis=1)
             cx = [jnp.concatenate([cx0 * (1.0 / math.cos(a))] * tiles, axis=1) for a in lats]
+            rest = [1.0 - (cx[r] + cy) for r in range(lat_count)]
             energy = [raw[rows, r * NLON : (r + 1) * NLON] * sea[r] for r in range(lat_count)]
-            for _ in range(ADV_STEPS):
+            for step in range(ADV_STEPS):
                 fresh = []
                 for r in range(lat_count):
                     e = energy[r]
                     side_x = pltpu.roll(e, 1 if east else NLON - 1, 1)
                     other = r - 1 if north else r + 1
-                    side_y = energy[other] if 0 <= other < lat_count else 0.0
-                    fresh.append((e - cx[r] * (e - side_x) - cy * (e - side_y)) * sea[r])
+                    value = rest[r] * e + cx[r] * side_x
+                    if 0 <= other < lat_count:
+                        value = value + cy * energy[other]
+                    fresh.append(value if step == ADV_STEPS - 1 else value * sea[r])
                 energy = fresh
             for r in range(lat_count):
                 moved[rows, r * NLON : (r + 1) * NLON] = energy[r]
@@ -357,61 +362,43 @@
             for f in range(begin, end):
                 y_copy(f, side_of(dy) * 2 + c, t).start()
 
-    def up_copy(slot, t):
-        return remote(
-            held.at[HALO + slot, :, lanes_of(t)],
-            held.at[HALO + slot - freq_group, :, lanes_of(t)],
-            z_sem.at[0], halo_sem.at[0, t], (zone + 1) % zones * group + rank,
-        )
-
-    def down_copy(slot, t):
-        return remote(
-            held.at[HALO + slot, :, lanes_of(t)],
-            held.at[HALO + slot + freq_group, :, lanes_of(t)],
-            z_sem.at[1], halo_sem.at[1, t], (zone + zones - 1) % zones * group + rank,
-        )
-
-    def early_up(f, c, t):
-        slot = rank * freq_dev + f
+    top = side > 0
+    early_way, late_way = jnp.where(top, 0, 1), jnp.where(top, 1, 0)
+    early_ok = jnp.where(top, zone < zones - 1, zone > 0)
+    late_ok = jnp.where(top, zone > 0, zone < zones - 1)
+    early_zone = jnp.where(top, zone + 1, zone + zones - 1) % zones
+    late_zone = jnp.where(top, zone + zones - 1, zone + 1) % zones
+    early_shift = HALO + jnp.where(top, -freq_group, freq_group)
+    late_shift = HALO + jnp.where(top, freq_group, -freq_group)
+
+    def early_slot(slot):
+        return early_ok & jnp.where(top, slot >= freq_group - HALO, slot < HALO)
+
+    def late_slot(slot):
+        return late_ok & jnp.where(top, slot < HALO, slot >= freq_group - HALO)
+
+    def early_copy(f, c, t):
         return remote(
             adv.at[f, :, tile_of(side * 2 + c, t)],
-            held.at[HALO + slot - freq_group, :, lanes_of(t)],
-            z_sem.at[0], halo_sem.at[0, t], (zone + 1) % zones * group + side * 2 + c,
-        )
-
-    def early_down(f, c, t):
-        slot = rank * freq_dev + f
-        return remote(
-            adv.at[f, :, tile_of(side * 2 + c, t)],
-            held.at[HALO + slot + freq_group, :, lanes_of(t)],
-            z_sem.at[1], halo_sem.at[1, t], (zone + zones - 1) % zones * group + side * 2 + c,
-        )
-
-    def goes_up(slot):
-        return (slot >= freq_group - HALO) & (zone < zones - 1)
-
-    def goes_down(slot):
-        return (slot < HALO) & (zone > 0)
+            held.at[early_shift + rank * freq_dev + f, :, lanes_of(t)],
+            z_sem.at[0], halo_sem.at[early_way, t], early_zone * group + side * 2 + c,
+        )
 
     def forward(slot, t):
-        @pl.when(goes_up(slot))
+        @pl.when(late_slot(slot))
         def _():
-            up_copy(slot, t).start()
-
-        @pl.when(goes_down(slot))
-        def _():
-            down_copy(slot, t).start()
+            remote(
+                held.at[HALO + slot, :, lanes_of(t)],
+                held.at[late_shift + slot, :, lanes_of(t)],
+                z_sem.at[1], halo_sem.at[late_way, t], late_zone * group + rank,
+            ).start()
 
     def send_near(t):
         for c in range(2):
             for f in range(freq_dev):
-                @pl.when(goes_up(rank * freq_dev + f))
+                @pl.when(early_slot(rank * freq_dev + f))
                 def _():
-                    early_up(f, c, t).start()
-
-                @pl.when(goes_down(rank * freq_dev + f))
-                def _():
-                    early_down(f, c, t).start()
+                    early_copy(f, c, t).start()
 
         for f in range(freq_dev):
             y_copy(f, rank_of((0, 1)), t).start()
@@ -445,13 +432,20 @@
             if level > 0:
                 signal(chain_sem.at[1], (me + count - group) % count)
 
+    def moment_copy(target_zone, target_rank):
+        return remote(
+            mom_out.at[:, :, cols_of(target_rank)], mom_in.at[me],
+            mom_send, mom_recv, target_zone * group + target_rank,
+        )
+
+    def send_zone_moments():
+        for step in range(1, group):
+            moment_copy(zone, (rank + step) % group).start()
+
     def send_moments():
-        for step in range(1, count):
-            target = (me + step) % count
-            remote(
-                mom_out.at[:, :, cols_of(target % group)], mom_in.at[me],
-                mom_send, mom_recv, target,
-            ).start()
+        for away in range(1, zones):
+            for other in range(group):
+                moment_copy((zone + away) % zones, other).start()
 
     far = list(range(1, sides))
     for dy in far:
@@ -485,28 +479,38 @@
     build(side)
     pack(0, 0, 0, freq_dev)
     send_near(0)
+    upper = zone >= zones // 2
     for t in range(1, parts):
+        last = t == parts - 1
         for dy in far:
             build(t * sides + side_of(dy))
             pack(t, dy, 0, freq_dev)
-            send_far(t, dy, 0, freq_dev)
+
+            @pl.when(jnp.logical_not(upper) if last else zone >= 0)
+            def _():
+                send_far(t, dy, 0, freq_dev)
         build(t * sides + side)
         pack(t, 0, 0, freq_dev)
+        if last:
+            up_relay(zones - 1)
+            down_relay(zones - 2)
+
+            send_zone_moments()
+
+            @pl.when(upper)
+            def _():
+                send_moments()
+                for dy in far:
+                    send_far(t, dy, 0, freq_dev)
+
         send_near(t)
-
-    up_relay(zones - 1)
-    down_relay(zones - 2)
-
-    @pl.when(zone >= zones // 2)
-    def _():
-        send_moments()
 
     for dy in far:
         arrive_group(dy, 0, 0, 1)
     for level in range(zones - 3, 0, -1):
         down_relay(level)
 
-    @pl.when((zone < zones // 2) & (zone > 0))
+    @pl.when(jnp.logical_not(upper) & (zone > 0))
     def _():
         send_moments()
 
@@ -527,12 +531,6 @@
 
     for dy in far:
         arrive_group(dy, 0, 1, freq_dev)
-    down_relay(0)
-
-    @pl.when(zone == 0)
-    def _():
-        send_moments()
-
     mom_in[me] = mom_out[:, :, cols_of(rank)]
     start = window_start(count, me, cells)
     near_ref[...] = place_ref[0:1, pl.ds(pl.multiple_of(start, LANES), WIDE)]
@@ -630,6 +628,13 @@
         for dy in range(1, sides):
             for dc in range(2):
                 ret_copy(rank_of((dy, dc)), t).start()
+        if t == 0:
+            down_relay(0)
+
+            @pl.when(zone == 0)
+            def _():
+                send_moments()
+
         if t < parts - 1:
             tally_rest(t)
 
@@ -679,28 +684,34 @@
 
     others = damp_in.at[0 : group - 1]
     remote(others, others, damp_send, damp_recv, (me + 1) % count).wait_recv()
-    for t in range(parts):
+
+    def finish(t):
         block = done.at[0 : (group - 1) * freq_dev, :, lanes_of(t)]
         remote(block, block, ret_send, ret_recv.at[t], (me + 1) % count).wait_recv()
-    for f in range(freq_dev):
-        omega = omega_of(me * freq_dev + f, (1, LANES))
-        for t in range(parts):
+        for f in range(freq_dev):
+            omega = omega_of(me * freq_dev + f, (1, LANES))
             for g in range(group):
                 cols = slice(block_of(g, t) * LANES, (block_of(g, t) + 1) * LANES)
                 value = back[f, :, cols] - (omega * damp_in[g, t, 0:1]) * adv[f, :, cols]
                 for i, piece in enumerate(split_bf16(value)):
                     split[(3 * f + i) * ND : (3 * f + i + 1) * ND, cols] = piece
-    for j in range(cells // WIDE):
-        low, high = max(0, j * WIDE - land), min(sea_cells, (j + 1) * WIDE)
-        cols = slice(j * WIDE, (j + 1) * WIDE)
-        got = jnp.dot(
-            split[:, low:high], spread_ref[low:high, cols], preferred_element_type=f32
-        )
-        for f in range(freq_dev):
-            base = 3 * f * ND
-            full_ref[f * ND : (f + 1) * ND, cols] = got[base : base + ND] + (
-                got[base + ND : base + 2 * ND]
-            ) + got[base + 2 * ND : base + 3 * ND]
+        ready = (t + 1) * group * LANES
+        for j in range(cells // WIDE):
+            low, high = max(0, j * WIDE - land), min(sea_cells, (j + 1) * WIDE)
+            if high > ready or high <= t * group * LANES:
+                continue
+            cols = slice(j * WIDE, (j + 1) * WIDE)
+            got = jnp.dot(
+                split[:, low:high], spread_ref[low:high, cols], preferred_element_type=f32
+            )
+            for f in range(freq_dev):
+                base = 3 * f * ND
+                full_ref[f * ND : (f + 1) * ND, cols] = got[base : base + ND] + (
+                    got[base + ND : base + 2 * ND]
+                ) + got[base + 2 * ND : base + 3 * ND]
+
+    for t in range(parts):
+        finish(t)
 
     block = held.at[0 : (group - 1) * freq_dev]
     remote(block, block, y_sem, held_sem.at[0, 0, 0], (me + 1) % count).wait_send()
@@ -716,26 +727,13 @@
         ).wait_send()
 
     for f in range(freq_dev):
-        @pl.when(goes_up(rank * freq_dev + f))
+        @pl.when(early_slot(rank * freq_dev + f))
         def _():
             drain(2, 0)
 
-        @pl.when(goes_down(rank * freq_dev + f))
-        def _():
-            drain(2, 1)
-
-    for dy in far:
-        for c in range(2):
-            for f in range(freq_dev):
-                slot = (side_of(dy) * 2 + c) * freq_dev + f
-
-                @pl.when(goes_up(slot))
-                def _():
-                    drain(1, 0)
-
-                @pl.when(goes_down(slot))
-                def _():
-                    drain(1, 1)
+    @pl.when(late_ok)
+    def _():
+        drain(HALO, 1)
 
     others = sum_in.at[0 : count - 1]
     remote(others, others, sum_send, sum_recv, (me + 1) % count).wait()
@@ -810,7 +808,7 @@
             pltpu.VMEM((cells,), f32),
             pltpu.VMEM((1, cells), f32),
             pltpu.VMEM((1, cells), f32),
-            pltpu.VMEM((sea_cells, cells), bf16),
+            pltpu.VMEM((sea_cells, cells), jnp.float8_e4m3fn),
             dma((3,)),
             pltpu.VMEM((bins_dev, cells), f32),
             pltpu.VMEM((bins_dev, cells), f32),

time: 18.7 us -> 17.9 us (0.957)
  Pallas kernels: 17.9 us -> 17.1 us
    pallas_call x1, Pallas kernels: 17 us -> 16.2 us  [fused_local(): pl.pallas_call(functools.partial(fused_kernel, count, group), out_shape=(...]
where the time goes in v6:
time: 17.9 us; the launch traced here: 17.7 us
  Pallas kernels  17.1 us (96%)
  between operations  0.64 us (4%)
    pallas_call x1, Pallas kernels, fused_local(): pl.pallas_call(functools.partial(fused_kernel, count, group), out_shape=(...  16.2 us
    pallas_call x1, Pallas kernels, fused_local(): pl.pallas_call(functools.partial(store_kernel, count), out_shape=(pltpu.H...  0.85 us

profile of v6, /device:TPU:0, one launch (start us, length us, event | category | flops | bytes accessed | tf_op | source)
XLA Modules:
  0.0 17.7 jit_solution(3766517543663158506)
XLA Ops:
  0.6 16.2 %shard_map.67 = (f32[96,1536]{1,0:T(8,128)S(1)}, f32[1,1024]{1,0:T(1,128)S(1)}, f32[1,256]{1,0:T(1,128)S(1)}) custom-call(s32[1536]{0:T(1024)} %sea_in.1, f32[1536]{0:T(1024)} %wind_in.1, f32[1536]{0:T(1024)} %angle_in.1, f32[96,1536]{1,0:T(8,128)} %spec_ref.1), custom_call_target="tpu_custom_call" | custom-call | tf_op jit(solution)/shard_map/pallas_call | solution.py:796
  16.9 0.9 %shard_map.68 = (f32[96,1536]{1,0:T(8,128)}, f32[96]{0:T(128)}, f32[1,1]{1,0:T(1,128)}) custom-call(f32[96,1536]{1,0:T(8,128)S(1)} %get-tuple-element.9.full_in, f32[1,1024]{1,0:T(1,128)S(1)} %get-tuple-element.10.height_in, f32[1,256]{1,0:T(1,128)S(1)} %get-tuple-element.11.near_in), custom_call_target="tpu_custom_call" | custom-call | tf_op jit(solution)/shard_map/pallas_call | solution.py:846

commit v7 on v6

--- a/solution.py
+++ b/solution.py
@@ -337,8 +337,10 @@
         return (side + dy) % sides
 
     def pack(t, dy, begin, end):
+        return packed(split.at[begin * 3 * ND : end * 3 * ND], t * sides + side_of(dy))
+
+    def unload(t, dy, begin, end, got):
         pair = t * sides + side_of(dy)
-        got = packed(split.at[begin * 3 * ND : end * 3 * ND], pair)
         cols = pl.ds(pl.multiple_of(pair * WIDE, LANES), WIDE)
         here = pl.ds(pl.multiple_of(side_of(dy) * WIDE, LANES), WIDE)
         mass, moment = None, None
@@ -452,7 +454,7 @@
         build(side_of(dy))
     advect(0)
     for dy in far:
-        pack(0, dy, 0, 1)
+        unload(0, dy, 0, 1, pack(0, dy, 0, 1))
     advect(1)
     pl.semaphore_wait(
         barrier, group - 1 + jnp.where(zone > 0, 2, 0) + jnp.where(zone < zones - 1, 2, 0)
@@ -471,30 +473,35 @@
     up_relay(1)
     for f in range(2, freq_dev):
         advect(f)
-    for dy in far:
-        pack(0, dy, 1, freq_dev)
-        send_far(0, dy, 1, freq_dev)
     for level in range(2, zones - 1):
         up_relay(level)
+    got = [pack(0, dy, 1, freq_dev) for dy in far]
     build(side)
-    pack(0, 0, 0, freq_dev)
+    got_near = pack(0, 0, 0, freq_dev)
+    for dy in far:
+        unload(0, dy, 1, freq_dev, got[dy - 1])
+        send_far(0, dy, 1, freq_dev)
+    unload(0, 0, 0, freq_dev, got_near)
     send_near(0)
+    down_relay(zones - 2)
     upper = zone >= zones // 2
     for t in range(1, parts):
         last = t == parts - 1
         for dy in far:
             build(t * sides + side_of(dy))
-            pack(t, dy, 0, freq_dev)
+        got = [pack(t, dy, 0, freq_dev) for dy in far]
+        build(t * sides + side)
+        got_near = pack(t, 0, 0, freq_dev)
+        for dy in far:
+            unload(t, dy, 0, freq_dev, got[dy - 1])
 
             @pl.when(jnp.logical_not(upper) if last else zone >= 0)
             def _():
                 send_far(t, dy, 0, freq_dev)
-        build(t * sides + side)
-        pack(t, 0, 0, freq_dev)
+
+        unload(t, 0, 0, freq_dev, got_near)
         if last:
             up_relay(zones - 1)
-            down_relay(zones - 2)
-
             send_zone_moments()
 
             @pl.when(upper)

time: 17.9 us -> 17.9 us (level)
  no operation moved by 1% of the time
where the time goes in v7:
time: 17.9 us; the launch traced here: 17.7 us
  Pallas kernels  17.1 us (96%)
  between operations  0.64 us (4%)
    pallas_call x1, Pallas kernels, fused_local(): pl.pallas_call(functools.partial(fused_kernel, count, group), out_shape=(...  16.2 us
    pallas_call x1, Pallas kernels, fused_local(): pl.pallas_call(functools.partial(store_kernel, count), out_shape=(pltpu.H...  0.85 us

profile of v7, /device:TPU:0, one launch (start us, length us, event | category | flops | bytes accessed | tf_op | source)
XLA Modules:
  0.0 17.7 jit_solution(991517596744450612)
XLA Ops:
  0.6 16.2 %shard_map.67 = (f32[96,1536]{1,0:T(8,128)S(1)}, f32[1,1024]{1,0:T(1,128)S(1)}, f32[1,256]{1,0:T(1,128)S(1)}) custom-call(s32[1536]{0:T(1024)} %sea_in.1, f32[1536]{0:T(1024)} %wind_in.1, f32[1536]{0:T(1024)} %angle_in.1, f32[96,1536]{1,0:T(8,128)} %spec_ref.1), custom_call_target="tpu_custom_call" | custom-call | tf_op jit(solution)/shard_map/pallas_call | solution.py:803
  16.9 0.9 %shard_map.68 = (f32[96,1536]{1,0:T(8,128)}, f32[96]{0:T(128)}, f32[1,1]{1,0:T(1,128)}) custom-call(f32[96,1536]{1,0:T(8,128)S(1)} %get-tuple-element.9.full_in, f32[1,1024]{1,0:T(1,128)S(1)} %get-tuple-element.10.height_in, f32[1,256]{1,0:T(1,128)S(1)} %get-tuple-element.11.near_in), custom_call_target="tpu_custom_call" | custom-call | tf_op jit(solution)/shard_map/pallas_call | solution.py:853

commit v8 on v7

--- a/solution.py
+++ b/solution.py
@@ -130,6 +130,7 @@
 LANES = 128
 WIDE = 256
 LAND = 4096.0
+UNROLL = 3
 
 
 def group_size(count, bins_dev, cells):
@@ -251,11 +252,11 @@
     def rank_of(offset):
         return (side + offset[0]) % sides * 2 + (core + offset[1]) % 2
 
-    def y_copy(f, peer, t):
+    def y_copy(begin, end, peer, t):
         return remote(
-            adv.at[f, :, tile_of(peer, t)],
-            held.at[HALO + rank * freq_dev + f, :, lanes_of(t)],
-            y_sem, held_sem.at[rank, f, t], zone * group + peer,
+            adv.at[begin:end, :, tile_of(peer, t)],
+            held.at[pl.ds(HALO + rank * freq_dev + begin, end - begin), :, lanes_of(t)],
+            y_sem, held_sem.at[rank, t], zone * group + peer,
         )
 
     dirs = lax.broadcasted_iota(jnp.int32, (ND, LANES), 0).astype(f32)
@@ -361,8 +362,7 @@
 
     def send_far(t, dy, begin, end):
         for c in range(2):
-            for f in range(begin, end):
-                y_copy(f, side_of(dy) * 2 + c, t).start()
+            y_copy(begin, end, side_of(dy) * 2 + c, t).start()
 
     top = side > 0
     early_way, late_way = jnp.where(top, 0, 1), jnp.where(top, 1, 0)
@@ -402,23 +402,23 @@
                 def _():
                     early_copy(f, c, t).start()
 
-        for f in range(freq_dev):
-            y_copy(f, rank_of((0, 1)), t).start()
+        y_copy(0, freq_dev, rank_of((0, 1)), t).start()
         for f in range(freq_dev):
             held[HALO + rank * freq_dev + f, :, lanes_of(t)] = adv[f, :, tile_of(rank, t)]
 
-    def arrive_group(dy, t, begin, end):
-        for f in range(begin, end):
-            for dc in range(2):
-                if (dy, dc) != (0, 0):
-                    source = rank_of((dy, dc))
-                    slot = source * freq_dev + f
-                    block = held.at[HALO + slot, :, lanes_of(t)]
-                    remote(
-                        block, block, y_sem, held_sem.at[source, f, t], (me + 1) % count
-                    ).wait_recv()
-                    if dy:
-                        forward(slot, t)
+    def arrive_group(dy, t):
+        for dc in range(2):
+            if (dy, dc) != (0, 0):
+                source = rank_of((dy, dc))
+                slots = held.at[
+                    pl.ds(HALO + source * freq_dev, freq_dev), :, lanes_of(t)
+                ]
+                remote(
+                    slots, slots, y_sem, held_sem.at[source, t], (me + 1) % count
+                ).wait_recv()
+                if dy and t < parts - 1:
+                    for f in range(freq_dev):
+                        forward(source * freq_dev + f, t)
 
     def up_relay(level):
         @pl.when(zone == level)
@@ -512,15 +512,6 @@
 
         send_near(t)
 
-    for dy in far:
-        arrive_group(dy, 0, 0, 1)
-    for level in range(zones - 3, 0, -1):
-        down_relay(level)
-
-    @pl.when(jnp.logical_not(upper) & (zone > 0))
-    def _():
-        send_moments()
-
     small[1].wait()
     small[2].wait()
     speed_all = wind_raw[...].reshape(1, cells)
@@ -536,13 +527,20 @@
         across = own[3:4] + own[4:5] + own[5:6]
         wind[:, t * LANES : (t + 1) * LANES] = cos_h * along + sin_h * across
 
+    for level in range(zones - 3, 0, -1):
+        down_relay(level)
+
+    @pl.when(jnp.logical_not(upper) & (zone > 0))
+    def _():
+        send_moments()
+
     for dy in far:
-        arrive_group(dy, 0, 1, freq_dev)
+        arrive_group(dy, 0)
     mom_in[me] = mom_out[:, :, cols_of(rank)]
     start = window_start(count, me, cells)
     near_ref[...] = place_ref[0:1, pl.ds(pl.multiple_of(start, LANES), WIDE)]
     for t in range(parts):
-        arrive_group(0, t, 0, freq_dev)
+        arrive_group(0, t)
 
     acc[...] = jnp.zeros_like(acc)
     ascending = side > 0
@@ -606,7 +604,7 @@
                 tally(energy, near, freq, t)
             return carry
 
-        lax.fori_loop(begin, end, source_step, 0)
+        lax.fori_loop(begin, end, source_step, 0, unroll=UNROLL)
 
     def tally_rest(t):
         def rest_step(i, carry):
@@ -621,7 +619,7 @@
             tally(energy, near, zone * freq_group + center, t)
             return carry
 
-        lax.fori_loop(0, half, rest_step, 0)
+        lax.fori_loop(0, half, rest_step, 0, unroll=UNROLL)
 
     half = freq_group // 2
     near_side = rank_of((0, 1))
@@ -635,6 +633,13 @@
         for dy in range(1, sides):
             for dc in range(2):
                 ret_copy(rank_of((dy, dc)), t).start()
+        if t == parts - 1:
+            for slot_rank in range(group):
+                for f in range(freq_dev):
+                    @pl.when(side != slot_rank // 2)
+                    def _():
+                        forward(slot_rank * freq_dev + f, t)
+
         if t == 0:
             down_relay(0)
 
@@ -684,7 +689,7 @@
     first_half(0)
     for t in range(1, parts):
         for dy in range(1, sides):
-            arrive_group(dy, t, 0, freq_dev)
+            arrive_group(dy, t)
         first_half(t)
         second_half(t - 1)
     second_half(parts - 1)
@@ -721,7 +726,7 @@
         finish(t)
 
     block = held.at[0 : (group - 1) * freq_dev]
-    remote(block, block, y_sem, held_sem.at[0, 0, 0], (me + 1) % count).wait_send()
+    remote(block, block, y_sem, held_sem.at[0, 0], (me + 1) % count).wait_send()
     remote(block, block, ret_send, ret_recv.at[0], (me + 1) % count).wait_send()
     others = mom_in.at[0 : count - 1]
     remote(others, others, mom_send, mom_recv, (me + 1) % count).wait_send()
@@ -834,7 +839,7 @@
             pltpu.VMEM((parts, 2, LANES), f32),
             pltpu.VMEM((group, parts, 2, LANES), f32),
             dma((freq_dev,)),
-            dma((group, freq_dev, parts)),
+            dma((group, parts)),
             dma((2, parts)),
             dma,
             dma((2,)),

time: 17.9 us -> 17.7 us (0.989)
  Pallas kernels: 17.1 us -> 16.9 us
    pallas_call x1, Pallas kernels: 16.2 us -> 16 us  [fused_local(): pl.pallas_call(functools.partial(fused_kernel, count, group), out_shape=(...]
where the time goes in v8:
time: 17.7 us; the launch traced here: 17.5 us
  Pallas kernels  16.9 us (95%)
  between operations  0.64 us (4%)
    pallas_call x1, Pallas kernels, fused_local(): pl.pallas_call(functools.partial(fused_kernel, count, group), out_shape=(...  16 us
    pallas_call x1, Pallas kernels, fused_local(): pl.pallas_call(functools.partial(store_kernel, count), out_shape=(pltpu.H...  0.85 us

profile of v8, /device:TPU:0, one launch (start us, length us, event | category | flops | bytes accessed | tf_op | source)
XLA Modules:
  0.0 17.5 jit_solution(1124100673833241978)
XLA Ops:
  0.6 16.0 %shard_map.67 = (f32[96,1536]{1,0:T(8,128)S(1)}, f32[1,1024]{1,0:T(1,128)S(1)}, f32[1,256]{1,0:T(1,128)S(1)}) custom-call(s32[1536]{0:T(1024)} %sea_in.1, f32[1536]{0:T(1024)} %wind_in.1, f32[1536]{0:T(1024)} %angle_in.1, f32[96,1536]{1,0:T(8,128)} %spec_ref.1), custom_call_target="tpu_custom_call" | custom-call | tf_op jit(solution)/shard_map/pallas_call | solution.py:808
  16.7 0.9 %shard_map.68 = (f32[96,1536]{1,0:T(8,128)}, f32[96]{0:T(128)}, f32[1,1]{1,0:T(1,128)}) custom-call(f32[96,1536]{1,0:T(8,128)S(1)} %get-tuple-element.9.full_in, f32[1,1024]{1,0:T(1,128)S(1)} %get-tuple-element.10.height_in, f32[1,256]{1,0:T(1,128)S(1)} %get-tuple-element.11.near_in), custom_call_target="tpu_custom_call" | custom-call | tf_op jit(solution)/shard_map/pallas_call | solution.py:858

commit v9 on v8

--- a/solution.py
+++ b/solution.py
@@ -386,8 +386,8 @@
             z_sem.at[0], halo_sem.at[early_way, t], early_zone * group + side * 2 + c,
         )
 
-    def forward(slot, t):
-        @pl.when(late_slot(slot))
+    def forward(slot, t, now):
+        @pl.when(late_slot(slot) & now)
         def _():
             remote(
                 held.at[HALO + slot, :, lanes_of(t)],
@@ -416,9 +416,9 @@
                 remote(
                     slots, slots, y_sem, held_sem.at[source, t], (me + 1) % count
                 ).wait_recv()
-                if dy and t < parts - 1:
+                if dy:
                     for f in range(freq_dev):
-                        forward(source * freq_dev + f, t)
+                        forward(source * freq_dev + f, t, t < parts - 1 or side == 0)
 
     def up_relay(level):
         @pl.when(zone == level)
@@ -634,11 +634,8 @@
             for dc in range(2):
                 ret_copy(rank_of((dy, dc)), t).start()
         if t == parts - 1:
-            for slot_rank in range(group):
-                for f in range(freq_dev):
-                    @pl.when(side != slot_rank // 2)
-                    def _():
-                        forward(slot_rank * freq_dev + f, t)
+            for slot in range(HALO):
+                forward(slot, t, side > 0)
 
         if t == 0:
             down_relay(0)
@@ -694,36 +691,56 @@
         second_half(t - 1)
     second_half(parts - 1)
 
+    def gather_back(t):
+        block = done.at[0 : (group - 1) * freq_dev, :, lanes_of(t)]
+        remote(block, block, ret_send, ret_recv.at[t], (me + 1) % count).wait_recv()
+        cols = slice(t * group * LANES, (t + 1) * group * LANES)
+        for f in range(freq_dev):
+            for i, piece in enumerate(split_bf16(back[f, :, cols])):
+                split[(3 * f + i) * ND : (3 * f + i + 1) * ND, cols] = piece
+
+    def spread(j, begin, end):
+        low, high = max(0, j * WIDE - land), min(sea_cells, (j + 1) * WIDE)
+        return jnp.dot(
+            split[begin:end, low:high],
+            spread_ref[low:high, j * WIDE : (j + 1) * WIDE],
+            preferred_element_type=f32,
+        )
+
+    def joined(got, f):
+        base = 3 * f * ND
+        return got[base : base + ND] + got[base + ND : base + 2 * ND] + (
+            got[base + 2 * ND : base + 3 * ND]
+        )
+
+    values = 3 * bins_dev
+    early_tiles = [
+        j for j in range(cells // WIDE) if (j + 1) * WIDE <= (parts - 1) * group * LANES
+    ]
+    for t in range(parts - 1):
+        gather_back(t)
+    for j in early_tiles:
+        got = spread(j, 0, values)
+        for f in range(freq_dev):
+            full_ref[f * ND : (f + 1) * ND, j * WIDE : (j + 1) * WIDE] = joined(got, f)
+    gather_back(parts - 1)
     others = damp_in.at[0 : group - 1]
     remote(others, others, damp_send, damp_recv, (me + 1) % count).wait_recv()
-
-    def finish(t):
-        block = done.at[0 : (group - 1) * freq_dev, :, lanes_of(t)]
-        remote(block, block, ret_send, ret_recv.at[t], (me + 1) % count).wait_recv()
+    for g in range(group):
+        for t in range(parts):
+            split[values:, block_of(g, t) * LANES : (block_of(g, t) + 1) * LANES] = rows_of(
+                split_bf16(damp_in[g, t, 0:1]), ND // 2, LANES
+            )
+    for j in range(cells // WIDE):
+        cols = slice(j * WIDE, (j + 1) * WIDE)
+        got = spread(j, values if j in early_tiles else 0, values + ND // 2)
+        rows = got[got.shape[0] - ND // 2 :]
+        row = rows[0:1] + rows[1:2] + rows[2:3]
         for f in range(freq_dev):
-            omega = omega_of(me * freq_dev + f, (1, LANES))
-            for g in range(group):
-                cols = slice(block_of(g, t) * LANES, (block_of(g, t) + 1) * LANES)
-                value = back[f, :, cols] - (omega * damp_in[g, t, 0:1]) * adv[f, :, cols]
-                for i, piece in enumerate(split_bf16(value)):
-                    split[(3 * f + i) * ND : (3 * f + i + 1) * ND, cols] = piece
-        ready = (t + 1) * group * LANES
-        for j in range(cells // WIDE):
-            low, high = max(0, j * WIDE - land), min(sea_cells, (j + 1) * WIDE)
-            if high > ready or high <= t * group * LANES:
-                continue
-            cols = slice(j * WIDE, (j + 1) * WIDE)
-            got = jnp.dot(
-                split[:, low:high], spread_ref[low:high, cols], preferred_element_type=f32
-            )
-            for f in range(freq_dev):
-                base = 3 * f * ND
-                full_ref[f * ND : (f + 1) * ND, cols] = got[base : base + ND] + (
-                    got[base + ND : base + 2 * ND]
-                ) + got[base + 2 * ND : base + 3 * ND]
-
-    for t in range(parts):
-        finish(t)
+            bins = slice(f * ND, (f + 1) * ND)
+            value = full_ref[bins, cols] if j in early_tiles else joined(got, f)
+            loss = omega_of(me * freq_dev + f, (1, WIDE)) * row
+            full_ref[bins, cols] = value - loss * moved[bins, cols]
 
     block = held.at[0 : (group - 1) * freq_dev]
     remote(block, block, y_sem, held_sem.at[0, 0], (me + 1) % count).wait_send()
@@ -824,7 +841,7 @@
             dma((3,)),
             pltpu.VMEM((bins_dev, cells), f32),
             pltpu.VMEM((bins_dev, cells), f32),
-            pltpu.VMEM((3 * bins_dev, cells), bf16),
+            pltpu.VMEM((3 * bins_dev + ND // 2, cells), bf16),
             pltpu.VMEM((ND // 2, cells), bf16),
             pltpu.VMEM((freq_dev, ND, sea_cells), f32),
             pltpu.VMEM((freq_group + 2 * HALO, ND, width), f32),

time: 17.7 us -> 17.5 us (0.989)
  Pallas kernels: 16.9 us -> 16.6 us
    pallas_call x1, Pallas kernels: 16 us -> 15.8 us  [fused_local(): pl.pallas_call(functools.partial(fused_kernel, count, group), out_shape=(...]
where the time goes in v9:
time: 17.5 us; the launch traced here: 17.3 us
  Pallas kernels  16.6 us (95%)
  between operations  0.64 us (4%)
    pallas_call x1, Pallas kernels, fused_local(): pl.pallas_call(functools.partial(fused_kernel, count, group), out_shape=(...  15.8 us
    pallas_call x1, Pallas kernels, fused_local(): pl.pallas_call(functools.partial(store_kernel, count), out_shape=(pltpu.H...  0.85 us

profile of v9, /device:TPU:0, one launch (start us, length us, event | category | flops | bytes accessed | tf_op | source)
XLA Modules:
  0.0 17.3 jit_solution(12423628864858911425)
XLA Ops:
  0.6 15.8 %shard_map.67 = (f32[96,1536]{1,0:T(8,128)S(1)}, f32[1,1024]{1,0:T(1,128)S(1)}, f32[1,256]{1,0:T(1,128)S(1)}) custom-call(s32[1536]{0:T(1024)} %sea_in.1, f32[1536]{0:T(1024)} %wind_in.1, f32[1536]{0:T(1024)} %angle_in.1, f32[96,1536]{1,0:T(8,128)} %spec_ref.1), custom_call_target="tpu_custom_call" | custom-call | tf_op jit(solution)/shard_map/pallas_call | solution.py:825
  16.4 0.9 %shard_map.68 = (f32[96,1536]{1,0:T(8,128)}, f32[96]{0:T(128)}, f32[1,1]{1,0:T(1,128)}) custom-call(f32[96,1536]{1,0:T(8,128)S(1)} %get-tuple-element.9.full_in, f32[1,1024]{1,0:T(1,128)S(1)} %get-tuple-element.10.height_in, f32[1,256]{1,0:T(1,128)S(1)} %get-tuple-element.11.near_in), custom_call_target="tpu_custom_call" | custom-call | tf_op jit(solution)/shard_map/pallas_call | solution.py:875

commit v10 on v9

--- a/solution.py
+++ b/solution.py
@@ -168,7 +168,7 @@
 
 
 def fused_kernel(
-    count, group, sea_in, wind_in, angle_in, spec_ref, full_ref, height_ref, near_ref,
+    count, group, sea_in, wind_in, angle_in, spec_ref, full_ref, mean_out, near_ref, loss_ref,
     sea_raw, wind_raw, angle_raw, aux_ref, place_ref, spread_ref, aux_sem,
     raw, moved, split, wsplit, adv, held, done, back, mom_out, mom_in, wind, acc,
     sum_out, sum_in, damp_out, damp_in,
@@ -696,8 +696,8 @@
         remote(block, block, ret_send, ret_recv.at[t], (me + 1) % count).wait_recv()
         cols = slice(t * group * LANES, (t + 1) * group * LANES)
         for f in range(freq_dev):
-            for i, piece in enumerate(split_bf16(back[f, :, cols])):
-                split[(3 * f + i) * ND : (3 * f + i + 1) * ND, cols] = piece
+            for i, piece in enumerate(split_bf16(back[f, :, cols])[:2]):
+                split[(2 * f + i) * ND : (2 * f + i + 1) * ND, cols] = piece
 
     def spread(j, begin, end):
         low, high = max(0, j * WIDE - land), min(sea_cells, (j + 1) * WIDE)
@@ -708,12 +708,10 @@
         )
 
     def joined(got, f):
-        base = 3 * f * ND
-        return got[base : base + ND] + got[base + ND : base + 2 * ND] + (
-            got[base + 2 * ND : base + 3 * ND]
-        )
-
-    values = 3 * bins_dev
+        base = 2 * f * ND
+        return got[base : base + ND] + got[base + ND : base + 2 * ND]
+
+    values = 2 * bins_dev
     early_tiles = [
         j for j in range(cells // WIDE) if (j + 1) * WIDE <= (parts - 1) * group * LANES
     ]
@@ -728,7 +726,10 @@
     remote(others, others, damp_send, damp_recv, (me + 1) % count).wait_recv()
     for g in range(group):
         for t in range(parts):
-            split[values:, block_of(g, t) * LANES : (block_of(g, t) + 1) * LANES] = rows_of(
+            loss_ref[0:1, block_of(g, t) * LANES : (block_of(g, t) + 1) * LANES] = damp_in[
+                g, t, 1:2
+            ]
+            split[values : values + ND // 2, block_of(g, t) * LANES : (block_of(g, t) + 1) * LANES] = rows_of(
                 split_bf16(damp_in[g, t, 0:1]), ND // 2, LANES
             )
     for j in range(cells // WIDE):
@@ -771,22 +772,24 @@
         for other in range(1, zones):
             mass = mass + sum_in[other * group + g]
         for t in range(parts):
-            mean = mass[:, t * LANES : (t + 1) * LANES] * (1.0 / (NF * ND)) - damp_in[g, t, 1:2]
             cols = slice(block_of(g, t) * LANES, (block_of(g, t) + 1) * LANES)
-            height_ref[0:1, cols] = 4.0 * jnp.sqrt(mean + 1e-06)
+            mean_out[0:1, cols] = mass[:, t * LANES : (t + 1) * LANES]
 
 
 def store_kernel(
-    count, full_in, height_in, near_in, new_out, wave_out, mean_out, wave_ref, mean_ref, sem
+    count, full_in, mass_in, near_in, loss_in, new_out, wave_out, mean_out,
+    height, wave_ref, mean_ref, sem,
 ):
     cells = full_in.shape[1]
-    sea_cells = height_in.shape[1]
+    sea_cells = mass_in.shape[1]
     copies = [
         pltpu.make_async_copy(full_in, new_out, sem.at[0]),
         pltpu.make_async_copy(wave_ref, wave_out, sem.at[1]),
         pltpu.make_async_copy(mean_ref, mean_out, sem.at[2]),
     ]
     copies[0].start()
+    mean = mass_in[...] * (1.0 / (NF * ND)) - loss_in[...]
+    height[...] = 4.0 * jnp.sqrt(mean + 1e-06)
     me = lax.axis_index("spec")
     points = cells // count
     shift = me * points - window_start(count, me, cells)
@@ -796,14 +799,14 @@
         place = place.astype(jnp.int32)
         wave = jnp.zeros((8, LANES), jnp.float32)
         for b in range(sea_cells // LANES):
-            values = jnp.broadcast_to(height_in[:, b * LANES : (b + 1) * LANES], (8, LANES))
+            values = jnp.broadcast_to(height[:, b * LANES : (b + 1) * LANES], (8, LANES))
             found = jnp.take_along_axis(values, place % LANES, axis=1)
             wave = jnp.where(place // LANES == b, found, wave)
         halves.append(wave)
     wave = jnp.concatenate(halves, axis=1)
     wave_ref[...] = pltpu.roll(wave, (WIDE - shift) % WIDE, 1)[0, :points]
     copies[1].start()
-    mean_ref[...] = jnp.sum(height_in[...], axis=1, keepdims=True) * (1.0 / sea_cells)
+    mean_ref[...] = jnp.sum(height[...], axis=1, keepdims=True) * (1.0 / sea_cells)
     copies[2].start()
     for copy in copies:
         copy.wait()
@@ -828,9 +831,10 @@
             pltpu.VMEM((bins_dev, cells), f32),
             pltpu.VMEM((1, sea_cells), f32),
             pltpu.VMEM((1, WIDE), f32),
+            pltpu.VMEM((1, sea_cells), f32),
         ),
         in_specs=[pl.BlockSpec(memory_space=pl.ANY)] * 4,
-        out_specs=(vmem,) * 3,
+        out_specs=(vmem,) * 4,
         scratch_shapes=[
             pltpu.VMEM((cells,), jnp.int32),
             pltpu.VMEM((cells,), f32),
@@ -879,9 +883,12 @@
             pltpu.HBM((points,), f32),
             pltpu.HBM((1, 1), f32),
         ),
-        in_specs=[vmem] * 3,
+        in_specs=[vmem] * 4,
         out_specs=(pl.BlockSpec(memory_space=pltpu.HBM),) * 3,
-        scratch_shapes=[pltpu.VMEM((points,), f32), pltpu.VMEM((1, 1), f32), dma((3,))],
+        scratch_shapes=[
+            pltpu.VMEM((1, sea_cells), f32), pltpu.VMEM((points,), f32),
+            pltpu.VMEM((1, 1), f32), dma((3,)),
+        ],
     )(*[pltpu.with_memory_space_constraint(piece, pltpu.VMEM) for piece in handed])
     return (out, wave, mean.reshape(1))
 

time: 17.5 us -> 17.4 us (level)
  no operation moved by 1% of the time
where the time goes in v10:
time: 17.4 us; the launch traced here: 17.2 us
  Pallas kernels  16.5 us (95%)
  between operations  0.64 us (4%)
    pallas_call x1, Pallas kernels, fused_local(): pl.pallas_call(functools.partial(fused_kernel, count, group), out_shape=(...  15.7 us
    pallas_call x1, Pallas kernels, fused_local(): pl.pallas_call(functools.partial(store_kernel, count), out_shape=(pltpu.H...  0.85 us

profile of v10, /device:TPU:0, one launch (start us, length us, event | category | flops | bytes accessed | tf_op | source)
XLA Modules:
  0.0 17.2 jit_solution(18407316316027503275)
XLA Ops:
  0.6 15.7 %shard_map.67 = (f32[96,1536]{1,0:T(8,128)S(1)}, f32[1,1024]{1,0:T(1,128)S(1)}, f32[1,256]{1,0:T(1,128)S(1)}, f32[1,1024]{1,0:T(1,128)S(1)}) custom-call(s32[1536]{0:T(1024)} %sea_in.1, f32[1536]{0:T(1024)} %wind_in.1, f32[1536]{0:T(1024)} %angle_in.1, f32[96,1536]{1,0:T(8,128)} %spec_ref.1), custom_call_target="tpu_custom_call" | custom-call | tf_op jit(solution)/shard_map/pallas_call | solution.py:828
  16.3 0.9 %shard_map.68 = (f32[96,1536]{1,0:T(8,128)}, f32[96]{0:T(128)}, f32[1,1]{1,0:T(1,128)}) custom-call(f32[96,1536]{1,0:T(8,128)S(1)} %get-tuple-element.10.full_in, f32[1,1024]{1,0:T(1,128)S(1)} %get-tuple-element.11.mass_in, f32[1,256]{1,0:T(1,128)S(1)} %get-tuple-element.12.near_in, f32[1,1024]{1,0:T(1,128)S(1)} %get-tuple-element.13.loss_in), custom_call_target="tpu_custom_call" | custom-call | tf_op jit(solution)/shard_map/pallas_call | solution.py:879

commit v11 on v10

--- a/solution.py
+++ b/solution.py
@@ -696,8 +696,8 @@
         remote(block, block, ret_send, ret_recv.at[t], (me + 1) % count).wait_recv()
         cols = slice(t * group * LANES, (t + 1) * group * LANES)
         for f in range(freq_dev):
-            for i, piece in enumerate(split_bf16(back[f, :, cols])[:2]):
-                split[(2 * f + i) * ND : (2 * f + i + 1) * ND, cols] = piece
+            for i, piece in enumerate(split_bf16(back[f, :, cols])):
+                split[(3 * f + i) * ND : (3 * f + i + 1) * ND, cols] = piece
 
     def spread(j, begin, end):
         low, high = max(0, j * WIDE - land), min(sea_cells, (j + 1) * WIDE)
@@ -708,10 +708,12 @@
         )
 
     def joined(got, f):
-        base = 2 * f * ND
-        return got[base : base + ND] + got[base + ND : base + 2 * ND]
-
-    values = 2 * bins_dev
+        base = 3 * f * ND
+        return got[base : base + ND] + got[base + ND : base + 2 * ND] + (
+            got[base + 2 * ND : base + 3 * ND]
+        )
+
+    values = 3 * bins_dev
     early_tiles = [
         j for j in range(cells // WIDE) if (j + 1) * WIDE <= (parts - 1) * group * LANES
     ]
@@ -729,7 +731,7 @@
             loss_ref[0:1, block_of(g, t) * LANES : (block_of(g, t) + 1) * LANES] = damp_in[
                 g, t, 1:2
             ]
-            split[values : values + ND // 2, block_of(g, t) * LANES : (block_of(g, t) + 1) * LANES] = rows_of(
+            split[values:, block_of(g, t) * LANES : (block_of(g, t) + 1) * LANES] = rows_of(
                 split_bf16(damp_in[g, t, 0:1]), ND // 2, LANES
             )
     for j in range(cells // WIDE):

time: 17.4 us -> 17.5 us (level)
  no operation moved by 1% of the time
where the time goes in v11:
time: 17.5 us; the launch traced here: 17.3 us
  Pallas kernels  16.6 us (95%)
  between operations  0.64 us (4%)
    pallas_call x1, Pallas kernels, fused_local(): pl.pallas_call(functools.partial(fused_kernel, count, group), out_shape=(...  15.8 us
    pallas_call x1, Pallas kernels, fused_local(): pl.pallas_call(functools.partial(store_kernel, count), out_shape=(pltpu.H...  0.85 us

profile of v11, /device:TPU:0, one launch (start us, length us, event | category | flops | bytes accessed | tf_op | source)
XLA Modules:
  0.0 17.3 jit_solution(14657062871582467027)
XLA Ops:
  0.6 15.8 %shard_map.67 = (f32[96,1536]{1,0:T(8,128)S(1)}, f32[1,1024]{1,0:T(1,128)S(1)}, f32[1,256]{1,0:T(1,128)S(1)}, f32[1,1024]{1,0:T(1,128)S(1)}) custom-call(s32[1536]{0:T(1024)} %sea_in.1, f32[1536]{0:T(1024)} %wind_in.1, f32[1536]{0:T(1024)} %angle_in.1, f32[96,1536]{1,0:T(8,128)} %spec_ref.1), custom_call_target="tpu_custom_call" | custom-call | tf_op jit(solution)/shard_map/pallas_call | solution.py:830
  16.4 0.9 %shard_map.68 = (f32[96,1536]{1,0:T(8,128)}, f32[96]{0:T(128)}, f32[1,1]{1,0:T(1,128)}) custom-call(f32[96,1536]{1,0:T(8,128)S(1)} %get-tuple-element.10.full_in, f32[1,1024]{1,0:T(1,128)S(1)} %get-tuple-element.11.mass_in, f32[1,256]{1,0:T(1,128)S(1)} %get-tuple-element.12.near_in, f32[1,1024]{1,0:T(1,128)S(1)} %get-tuple-element.13.loss_in), custom_call_target="tpu_custom_call" | custom-call | tf_op jit(solution)/shard_map/pallas_call | solution.py:881
